TPU v7x, 8 devices: a whole 2x2x1 slice. The times are simulated.
8 devices in a mesh: data: 1 (over z), cols: 2 (over y), model: 4 (over x, core).
Axes of the slice: x: 2, y: 2, z: 1, core: 2. Of those that a mesh axis runs over, the one named last changes fastest.
Arguments:
- x_in: bfloat16 [32, 64, 128, 256], P('data', None, 'cols', 'model')
- w_conv1: bfloat16 [3, 3, 256, 512], P(None, None, 'model')
- b_conv1: float32 [512], replicated
- w_conv2: bfloat16 [3, 3, 512, 512], replicated
- b_conv2: float32 [512], replicated
Outputs:
- output: float32 [32, 64, 128, 512], P('data', 'model', 'cols')
All inputs are finite; a program needn't handle non-finite values.
Results may differ from a plain program's by a relative error of at most 0.00994635.
Values are sent between devices in bfloat16 or wider.
A program may use at most 1 GiB of HBM per device.

v0:
```python
import jax
import jax.numpy as jnp
from jax import lax
from jax.sharding import PartitionSpec as P

CONV_DIMS = ('NHWC', 'HWIO', 'NHWC')


def col_border(block, cols_size):
    from_left = lax.ppermute(block[:, :, -1:, :], 'cols', [(source, source + 1) for source in range(cols_size - 1)])
    from_right = lax.ppermute(block[:, :, :1, :], 'cols', [(source + 1, source) for source in range(cols_size - 1)])
    return jnp.concatenate([from_left, block, from_right], axis=2)


def solution(mesh):
    cols_size = mesh.shape['cols']
    model_size = mesh.shape['model']

    def local_step(x_loc, w1_loc, b_conv1, w_conv2, b_conv2):
        images = x_loc.shape[0]
        height = x_loc.shape[1]
        width_loc = x_loc.shape[2]
        chan_mid = w1_loc.shape[3]
        rows_dev = height // model_size
        x_wide = col_border(x_loc, cols_size)
        part_sum = lax.conv_general_dilated(x_wide, w1_loc, (1, 1), ((1, 1), (0, 0)), dimension_numbers=CONV_DIMS, preferred_element_type=jnp.float32)
        part_pad = jnp.pad(part_sum.astype(jnp.bfloat16), ((0, 0), (1, 1), (0, 0), (0, 0)))
        top_rows = part_pad[:, 0:height:rows_dev][:, :, None]
        bottom_rows = part_pad[:, rows_dev + 1::rows_dev][:, :, None]
        inner_rows = part_pad[:, 1:height + 1].reshape(images, model_size, rows_dev, width_loc, chan_mid)
        tiles = jnp.concatenate([top_rows, inner_rows, bottom_rows], axis=2)
        tile_sum = lax.psum_scatter(tiles, 'model', scatter_dimension=1, tiled=False)
        first_row = lax.axis_index('model') * rows_dev - 1
        row_pos = first_row + jnp.arange(rows_dev + 2)
        inside = ((row_pos >= 0) & (row_pos < height))[:, None, None]
        hidden = jnp.where(inside, jnp.maximum(tile_sum.astype(jnp.float32) + b_conv1, 0.0), 0.0).astype(jnp.bfloat16)
        hidden_wide = col_border(hidden, cols_size)
        result = lax.conv_general_dilated(hidden_wide, w_conv2, (1, 1), 'VALID', dimension_numbers=CONV_DIMS, preferred_element_type=jnp.float32)
        return result + b_conv2

    return jax.shard_map(local_step, mesh=mesh, in_specs=(P('data', None, 'cols', 'model'), P(None, None, 'model', None), P(), P(), P()), out_specs=P('data', 'model', 'cols', None), check_vma=False)
```

profile of v0, /device:TPU:0, one launch (start us, length us, event | category | flops | bytes accessed | tf_op | source)
XLA Modules:
  0.0 1530.0 jit_solution(4881018210791893768)
XLA Ops:
  6.5 0.0 copy-start
  6.5 0.0 reduce-scatter.4.cloned.1.call-start
  6.5 30.5 %copy.12 = bf16[32,64,64,64]{3,0,2,1:T(8,128)(2,1)} copy(bf16[32,64,64,64]{3,2,1,0:T(8,128)(2,1)} %param.5) | data formatting | bytes 33554432 | tf_op args[0]
  37.0 1.3 fusion.21
  38.3 5.3 collective-permute-start
  43.6 1.5 collective-permute-start.1
  45.2 9.6 collective-permute-done
  54.7 4.2 collective-permute-done.1
  58.9 0.0 copy-done
  58.9 116.8 %convolution_convert_fusion = bf16[32,64,64,512]{3,0,2,1:T(8,128)(2,1)} fusion(bf16[3,3,64,512]{3,2,1,0:T(8,128)(2,1)S(1)} %copy-done, bf16[32,64,1,64]{3,0,2,1:T(8,128)(2,1)S(1)} %collective-permute-done.1, bf16[32,64,64,64]{3,0,2,1:T(8,128)(2,1)} %copy.12, bf16[32,64,1,64]{3,0,2,1:T(8,128)(2,1)S(1)} %collective-permute-done), kind=kOutput, calls=%fused_computation.3 | convolution fusion | flops 76623118336 | bytes 152109056 | tf_op jit(solution)/shard_map/conv_general_dilated | solution.py:26
  175.7 10.9 fusion.16
  186.6 96.6 %pad_maximum_fusion = bf16[32,4,18,64,512]{4,0,3,2,1:T(8,128)(2,1)} fusion(bf16[32,4,1,64,512]{4,0,3,2,1:T(8,128)(2,1)} %get-tuple-element.6, bf16[32,4,16,64,512]{4,0,3,2,1:T(8,128)(2,1)} %bitcast.2, bf16[32,4,1,64,512]{4,0,3,2,1:T(8,128)(2,1)} %get-tuple-element.5), kind=kLoop, calls=%fused_computation | loop fusion | flops 150994944 | bytes 301989888 | tf_op jit(solution)/shard_map/concatenate | solution.py:31
  283.2 0.0 copy-start.2
  283.3 0.0 reduce-scatter.4.cloned.1.call-update
  283.3 0.0 copy-start.3
  283.3 970.2 %reduce-scatter.4.cloned.1.call-done = bf16[32,1,18,64,512]{4,0,3,2,1:T(8,128)(2,1)} async-done(((bf16[32,4,18,64,512]{4,0,3,2,1:T(8,128)(2,1)}), bf16[32,1,18,64,512]{4,0,3,2,1:T(8,128)(2,1)}) %reduce-scatter.4.cloned.1.call-update) | async-done | bytes 37748752
  1253.5 0.0 copy-done.2
  1253.5 25.8 %fusion.2 = bf16[32,18,64,512]{3,0,2,1:T(8,128)(2,1)} fusion(bf16[32,1,18,64,512]{4,0,3,2,1:T(8,128)(2,1)} %reduce-scatter.4.cloned.1.call-done, f32[512]{0:T(512)S(1)} %copy-done.2, pred[18]{0:T(512)(128)(4,1)S(1)} %compare_and_fusion), kind=kLoop, calls=%fused_computation.7 | loop fusion | flops 94371840 | bytes 75499536 | tf_op jit(solution)/shard_map/convert_element_type | solution.py:36
  1279.4 1.3 fusion.20
  1280.7 3.4 collective-permute-start.2
  1284.1 1.3 collective-permute-start.3
  1285.4 10.9 collective-permute-done.2
  1296.4 4.2 collective-permute-done.3
  1300.6 0.0 copy-done.3
  1300.6 0.0 copy-start.1
  1300.6 165.9 %broadcast_add_fusion = f32[32,16,64,512]{3,0,2,1:T(8,128)} fusion(f32[512]{0:T(512)S(1)} %copy-done.3, bf16[3,3,512,512]{3,2,1,0:T(8,128)(2,1)} %param.8, bf16[32,18,1,512]{3,0,2,1:T(8,128)(2,1)S(1)} %collective-permute-done.3, bf16[32,18,64,512]{3,0,2,1:T(8,128)(2,1)} %fusion.2, bf16[32,18,1,512]{3,0,2,1:T(8,128)(2,1)S(1)} %collective-permute-done.2), kind=kOutput, calls=%fused_computation.19 | convolution fusion | flops 154674528256 | bytes 110757888 | tf_op jit(solution)/shard_map/conv_general_dilated | solution.py:38
  1466.5 56.5 %copy.17 = f32[32,16,64,512]{3,2,1,0:T(8,128)} copy(f32[32,16,64,512]{3,0,2,1:T(8,128)} %broadcast_add_fusion) | data formatting | bytes 134217728 | tf_op jit(solution)/shard_map/add | solution.py:39
  1523.0 0.0 copy-done.1
  (1 shorter events, 0.0 us)
Async XLA Ops:
  6.5 52.4 %copy-start = (bf16[3,3,64,512]{3,2,1,0:T(8,128)(2,1)S(1)}, bf16[3,3,64,512]{3,2,1,0:T(8,128)(2,1)}, u32[]{:S(2)}) copy-start(bf16[3,3,64,512]{3,2,1,0:T(8,128)(2,1)} %param.6) | copy-start | bytes 1769476
  6.5 1247.0 %reduce-scatter.4.cloned.1.call-start = ((), (), s32[]{:S(2)}) async-start(), calls=%async_computation.1 | async-start | bytes 188743680
  38.3 16.4 %collective-permute-start = (bf16[32,64,1,64]{3,0,2,1:T(8,128)(2,1)S(1)}, bf16[32,64,1,64]{3,0,2,1:T(8,128)(2,1)S(1)}, u32[]{:S(2)}, u32[]{:S(2)}) collective-permute-start(bf16[32,64,1,64]{3,0,2,1:T(8,128)(2,1)S(1)} %get-tuple-element.9), channel_id=1, source_target_pairs={{0,4},{1,5},{2,6},{3,7}} | collective-permute-start | bytes 786440 | tf_op jit(solution)/shard_map/ppermute | solution.py:10
  43.6 15.3 collective-permute-start.1
  283.2 970.3 %copy-start.2 = (f32[512]{0:T(512)S(1)}, f32[512]{0:T(512)}, u32[]{:S(2)}) copy-start(f32[512]{0:T(512)} %param.7) | copy-start | bytes 6148
  283.3 1017.3 %copy-start.3 = (f32[512]{0:T(512)S(1)}, f32[512]{0:T(512)}, u32[]{:S(2)}) copy-start(f32[512]{0:T(512)} %param.9) | copy-start | bytes 6148
  1280.7 15.7 %collective-permute-start.2 = (bf16[32,18,1,512]{3,0,2,1:T(8,128)(2,1)S(1)}, bf16[32,18,1,512]{3,0,2,1:T(8,128)(2,1)S(1)}, u32[]{:S(2)}, u32[]{:S(2)}) collective-permute-start(bf16[32,18,1,512]{3,0,2,1:T(8,128)(2,1)S(1)} %get-tuple-element.7), channel_id=1, source_target_pairs={{0,4},{1,5},{2,6},{3,7}} | collective-permute-start | bytes 1769480 | tf_op jit(solution)/shard_map/ppermute | solution.py:10
  1284.1 16.4 %collective-permute-start.3 = (bf16[32,18,1,512]{3,0,2,1:T(8,128)(2,1)S(1)}, bf16[32,18,1,512]{3,0,2,1:T(8,128)(2,1)S(1)}, u32[]{:S(2)}, u32[]{:S(2)}) collective-permute-start(bf16[32,18,1,512]{3,0,2,1:T(8,128)(2,1)S(1)} %get-tuple-element.8), channel_id=1, source_target_pairs={{4,0},{5,1},{6,2},{7,3}} | collective-permute-start | bytes 1769480 | tf_op jit(solution)/shard_map/ppermute | solution.py:11
  1300.6 222.4 %copy-start.1 = (bf16[3,3,64,512]{3,2,1,0:T(8,128)(2,1)S(1)}, bf16[3,3,64,512]{3,2,1,0:T(8,128)(2,1)}, u32[]{:S(2)}) copy-start(bf16[3,3,64,512]{3,2,1,0:T(8,128)(2,1)} %param.6) | copy-start | bytes 1769476
Sparse Core Ops, SparseCore 0:
  283.4 970.0 reduce-scatter.3
where the time goes:
time: 1530 us
  waiting for transfers between devices  999 us (65%)
  matrix products  283 us (18%)
  other arithmetic  122 us (8%)
  local copies, waits for them, and re-layouts  101 us (7%)
    unnamed x2, waiting for transfers between devices  970 us
    conv_general_dilated x1, matrix products, local_step(): lax.conv_general_dilated(hidden_wide, w_conv2, (1, 1), 'VALID', dimension...  166 us
    conv_general_dilated x1, matrix products, local_step(): lax.conv_general_dilated(x_wide, w1_loc, (1, 1), ((1, 1), (0, 0)), dimens...  117 us
    concatenate x1, other arithmetic, local_step(): tiles = jnp.concatenate([top_rows, inner_rows, bottom_rows], axis=2)  96.6 us
    add x1, local copies, waits for them, and re-layouts, local_step(): return result + b_conv2  56.5 us
  transfers between devices with their start and end apart: 5, of which 5 were waited for; matrix products, arithmetic and copies ran while one was open for 0% of the time, Pallas kernels for 0%

commit v1 on v0

v1 whole, which is shorter than its diff:
```python
import functools

import jax
import jax.numpy as jnp
from jax import lax
from jax.experimental import pallas as pl
from jax.experimental.pallas import tpu as pltpu
from jax.sharding import PartitionSpec as P

ROWS = 16
COLS = 64
WIN = 20


def shift_down(v, edge):
    rolled = pltpu.roll(v, 1, axis=0)
    pos = lax.broadcasted_iota(jnp.int32, v.shape, 0) % COLS
    return jnp.where(pos == 0, edge, rolled)


def shift_up(v, edge):
    rolled = pltpu.roll(v, v.shape[0] - 1, axis=0)
    pos = lax.broadcasted_iota(jnp.int32, v.shape, 0) % COLS
    return jnp.where(pos == COLS - 1, edge, rolled)


def build_x3(is_left, xc, hx, x3, xh):
    for half in range(2):
        lane = half * 128
        for r in range(WIN):
            v = xc[half, r].astype(jnp.float32)
            h = hx[half, r].astype(jnp.float32)
            near = jnp.where(is_left, h[0:1], h[15:16])
            far = jnp.where(is_left, h[1:2], h[14:15])
            own = jnp.where(is_left, v[COLS - 1:COLS], v[0:1])
            zero = jnp.zeros_like(near)
            rows = pl.ds(r * COLS, COLS)
            x3[rows, lane:lane + 128] = shift_down(v, jnp.where(is_left, zero, near)).astype(jnp.bfloat16)
            x3[rows, 256 + lane:384 + lane] = xc[half, r]
            x3[rows, 512 + lane:640 + lane] = shift_up(v, jnp.where(is_left, near, zero)).astype(jnp.bfloat16)
            xh[r:r + 1, lane:lane + 128] = jnp.where(is_left, own, far)
            xh[r:r + 1, 256 + lane:384 + lane] = near
            xh[r:r + 1, 512 + lane:640 + lane] = jnp.where(is_left, far, own)


def conv1(is_left, top, bottom, x3, xh, w1, b1, y3, blocks=((0, 10), (10, 8))):
    edge_all = None
    for first, count in blocks:
        m = count * COLS
        lhs = jnp.concatenate([x3[(first + dy) * COLS:(first + dy) * COLS + m, :] for dy in range(3)], axis=1)
        if first == 0:
            edge = jnp.concatenate([xh[dy:dy + 32, :] for dy in range(3)], axis=1).astype(jnp.bfloat16)
            lhs = jnp.concatenate([edge, lhs], axis=0)
        z = jnp.dot(lhs, w1[...], preferred_element_type=jnp.float32)
        z = jnp.maximum(z + b1[...], 0.0)
        if first == 0:
            edge_all = z[:32]
            z = z[32:]
        for r in range(count):
            row = first + r
            v = z[r * COLS:(r + 1) * COLS]
            e = edge_all[row:row + 1]
            if row == 0:
                v = jnp.where(top, 0.0, v)
                e = jnp.where(top, 0.0, e)
            if row == ROWS + 1:
                v = jnp.where(bottom, 0.0, v)
                e = jnp.where(bottom, 0.0, e)
            zero = jnp.zeros_like(e)
            dst = pl.ds(row * COLS, COLS)
            y3[dst, 0:512] = shift_down(v, jnp.where(is_left, zero, e)).astype(jnp.bfloat16)
            y3[dst, 512:1024] = v.astype(jnp.bfloat16)
            y3[dst, 1024:1536] = shift_up(v, jnp.where(is_left, e, zero)).astype(jnp.bfloat16)


def conv2(y3, w2, b2, out, blk=8):
    for first in range(0, ROWS, blk):
        m = blk * COLS
        lhs = jnp.concatenate([y3[(first + dy) * COLS:(first + dy) * COLS + m, :] for dy in range(3)], axis=1)
        out[first * COLS:first * COLS + m, :] = jnp.dot(lhs, w2[...], preferred_element_type=jnp.float32) + b2[...]


def compute_kernel(xg, hx, w1, b1, w2, b2, out, x3, xh, y3):
    model = lax.axis_index('model')
    is_left = lax.axis_index('cols') == 0

    @pl.when(pl.program_id(0) == 0)
    def _():
        xh[...] = jnp.zeros_like(xh)

    build_x3(is_left, xg.at[0], hx.at[0], x3, xh)
    conv1(is_left, model == 0, model == 3, x3, xh, w1, b1, y3)
    conv2(y3, w2, b2, out.at[0])


def compute(xg, hx, w1, b1, w2, b2):
    images = xg.shape[0]
    full = lambda shape: pl.BlockSpec(shape, lambda n: (0,) * len(shape))
    return pl.pallas_call(
        compute_kernel,
        grid=(images,),
        out_shape=jax.ShapeDtypeStruct((images, ROWS * COLS, 512), jnp.float32),
        in_specs=[
            pl.BlockSpec((1, 2, WIN, COLS, 128), lambda n: (n, 0, 0, 0, 0)),
            pl.BlockSpec((1, 2, WIN, 16, 128), lambda n: (n, 0, 0, 0, 0)),
            full((2304, 512)), full((1, 512)), full((4608, 512)), full((1, 512)),
        ],
        out_specs=pl.BlockSpec((1, ROWS * COLS, 512), lambda n: (n, 0, 0)),
        scratch_shapes=[
            pltpu.VMEM((WIN * COLS, 768), jnp.bfloat16),
            pltpu.VMEM((40, 768), jnp.float32),
            pltpu.VMEM(((ROWS + 2) * COLS, 1536), jnp.bfloat16),
        ],
        compiler_params=pltpu.CompilerParams(vmem_limit_bytes=60 * 1024 * 1024),
    )(xg, hx, w1, b1, w2, b2)


def solution(mesh):
    def local_step(x, w1, b1, w2, b2):
        images = x.shape[0]
        wide = jnp.pad(x, ((0, 0), (2, 2), (0, 0), (0, 0)))
        tiles = jnp.stack([wide[:, ROWS * k:ROWS * k + WIN] for k in range(4)])
        got = lax.all_to_all(tiles, 'model', 0, 0)
        got = got.reshape(2, 2, images, WIN, COLS, 64)
        xg = got.transpose(2, 0, 3, 4, 1, 5).reshape(images, 2, WIN, COLS, 128)
        is_left = lax.axis_index('cols') == 0
        edge = jnp.where(is_left, xg[:, :, :, 48:64], xg[:, :, :, 0:16])
        hx = lax.ppermute(edge, 'cols', [(0, 1), (1, 0)])
        w1g = lax.all_gather(w1, 'model', axis=2, tiled=True).reshape(2304, 512)
        y = compute(xg, hx, w1g, b1.reshape(1, 512), w2.reshape(4608, 512), b2.reshape(1, 512))
        return y.reshape(images, ROWS, COLS, 512)

    return jax.shard_map(local_step, mesh=mesh, in_specs=(P('data', None, 'cols', 'model'), P(None, None, 'model', None), P(), P(), P()), out_specs=P('data', 'model', 'cols', None), check_vma=False)
```

time: 1530 us -> 954 us (0.62)
  waiting for transfers between devices: 999 us -> 341 us
  matrix products: 283 us -> 0 us
  Pallas kernels: 0 us -> 260 us
  local copies, waits for them, and re-layouts: 101 us -> 292 us
  other arithmetic: 122 us -> 35.4 us
    unnamed x2 -> x1, waiting for transfers between devices: 970 us -> 0.02 us
    conv_general_dilated x2 -> x0, matrix products: 283 us -> none  [the longest x1 166 us: local_step(): lax.conv_general_dilated(hidden_wide, w_conv2, (1, 1), 'VALID', dimension...]
    pallas_call x0 -> x1, Pallas kernels: none -> 260 us  [compute(): pl.pallas_call(compute_kernel, grid=(images,), out_shape=jax.ShapeDtypeSt...]
    all_to_all x0 -> x1, waiting for transfers between devices: none -> 228 us  [local_step(): got = lax.all_to_all(tiles, 'model', 0, 0)]
    reshape x0 -> x2, local copies, waits for them, and re-layouts: none -> 140 us  [the longest x1 75.3 us: local_step(): got = got.reshape(2, 2, images, WIN, COLS, 64)]
    concatenate x1 -> x0, other arithmetic: 96.6 us -> none  [local_step(): tiles = jnp.concatenate([top_rows, inner_rows, bottom_rows], axis=2)]
    unnamed x9 -> x2, local copies, waits for them, and re-layouts: 30.5 us -> 115 us
    ppermute x4 -> x1, waiting for transfers between devices: 28.8 us -> 92.8 us  [local_step(): hx = lax.ppermute(edge, 'cols', [(0, 1), (1, 0)])]
  transfers between devices with their start and end apart: 5 -> 3, of which waited for: 5 -> 3; matrix products, arithmetic and copies ran while one was open for 0% -> 0% of each run, Pallas kernels for 0% -> 0%
where the time goes in v1:
time: 954 us; the launch traced here: 952 us
  waiting for transfers between devices  341 us (36%)
  local copies, waits for them, and re-layouts  292 us (31%)
  Pallas kernels  260 us (27%)
  other arithmetic  35.4 us (4%)
  between operations  13.4 us (1%)
  starting transfers between devices  10.3 us (1%)
    pallas_call x1, Pallas kernels, compute(): pl.pallas_call(compute_kernel, grid=(images,), out_shape=jax.ShapeDtypeSt...  260 us
    all_to_all x1, waiting for transfers between devices, local_step(): got = lax.all_to_all(tiles, 'model', 0, 0)  228 us
    unnamed x2, local copies, waits for them, and re-layouts  115 us
    ppermute x1, waiting for transfers between devices, local_step(): hx = lax.ppermute(edge, 'cols', [(0, 1), (1, 0)])  92.8 us
    reshape x1, local copies, waits for them, and re-layouts, local_step(): got = got.reshape(2, 2, images, WIN, COLS, 64)  75.3 us
    reshape x1, local copies, waits for them, and re-layouts, local_step(): xg = got.transpose(2, 0, 3, 4, 1, 5).reshape(images, 2, WIN, COLS, 128)  65.2 us
    another operation x1, local copies, waits for them, and re-layouts, local_step(): tiles = jnp.stack([wide[:, ROWS * k:ROWS * k + WIN] for k in range(4)])  36.2 us
    another operation x1, other arithmetic, local_step(): tiles = jnp.stack([wide[:, ROWS * k:ROWS * k + WIN] for k in range(4)])  28.4 us
  transfers between devices with their start and end apart: 3, of which 3 were waited for; matrix products, arithmetic and copies ran while one was open for 0% of the time, Pallas kernels for 0%

profile of v1, /device:TPU:0, one launch (start us, length us, event | category | flops | bytes accessed | tf_op | source)
XLA Modules:
  0.0 952.2 jit_solution(14553220628625834046)
XLA Ops:
  6.5 36.2 %fusion = (bf16[1,32,20,64,64]{4,3,2,1,0:T(8,128)(2,1)}, bf16[1,32,20,64,64]{4,3,2,1,0:T(8,128)(2,1)}, bf16[1,32,20,64,64]{4,3,2,1,0:T(8,128)(2,1)}, bf16[1,32,20,64,64]{4,3,2,1,0:T(8,128)(2,1)}) fusion(bf16[32,64,64,64]{3,2,1,0:T(8,128)(2,1)} %param.5), kind=kLoop, calls=%fused_computation.4 | loop fusion | bytes 75497472 | tf_op jit(solution)/shard_map/stack | solution.py:122
  42.7 28.4 %pad_maximum_fusion = bf16[4,32,20,64,64]{4,3,2,1,0:T(8,128)(2,1)} fusion(bf16[1,32,20,64,64]{4,3,2,1,0:T(8,128)(2,1)} %get-tuple-element.6, bf16[1,32,20,64,64]{4,3,2,1,0:T(8,128)(2,1)} %get-tuple-element.7, bf16[1,32,20,64,64]{4,3,2,1,0:T(8,128)(2,1)} %get-tuple-element.8, bf16[1,32,20,64,64]{4,3,2,1,0:T(8,128)(2,1)} %get-tuple-element.5), kind=kLoop, calls=%fused_computation | loop fusion | flops 31457280 | bytes 41943040 | tf_op jit(solution)/shard_map/stack | solution.py:122
  71.1 57.9 %reshape.28 = bf16[4,2,1310720]{2,1,0:T(2,128)(2,1)} reshape(bf16[4,32,20,64,64]{4,3,2,1,0:T(8,128)(2,1)} %pad_maximum_fusion) | data formatting | bytes 41943040
  129.0 7.7 all-to-all-start
  136.7 0.2 all-gather.2.cloned.1.call-start
  136.9 228.4 %all-to-all-done = bf16[4,2,1310720]{2,1,0:T(2,128)(2,1)} async-done(((bf16[4,2,1310720]{2,1,0:T(2,128)(2,1)}), bf16[4,2,1310720]{2,1,0:T(2,128)(2,1)}, u32[]{:S(2)}, u32[]{:S(2)}) %all-to-all-start) | async-done | bytes 20971552 | tf_op jit(solution)/shard_map/all_to_all | solution.py:123
  365.3 57.3 %reshape.29 = bf16[4,32,20,64,64]{4,3,2,1,0:T(8,128)(2,1)} reshape(bf16[4,2,1310720]{2,1,0:T(2,128)(2,1)} %all-to-all-done) | data formatting | bytes 41943040
  422.6 75.3 %copy.8 = bf16[2,2,32,20,64,64]{5,1,4,3,0,2:T(2,128)(2,1)} copy(bf16[2,2,32,20,64,64]{5,4,3,2,1,0:T(8,128)(2,1)} %bitcast.17) | data formatting | bytes 41943040 | tf_op jit(solution)/shard_map/reshape | solution.py:124
  497.9 65.2 %reshape.22.xg = bf16[32,2,20,64,128]{4,3,2,1,0:T(8,128)(2,1)} reshape(bf16[32,2,20,64,2,64]{5,4,3,2,1,0:T(2,128)(2,1)} %bitcast.18) | data formatting | bytes 41943040 | tf_op jit(solution)/shard_map/reshape | solution.py:125
  563.1 7.0 slice_select_fusion
  570.1 2.4 collective-permute-start
  572.4 0.0 all-gather.2.cloned.1.call-update
  572.5 20.0 %all-gather.2.cloned.1.call-done = bf16[3,3,256,512]{3,2,1,0:T(8,128)(2,1)} async-done(((bf16[3,3,64,512]{3,2,1,0:T(8,128)(2,1)}), bf16[3,3,256,512]{3,2,1,0:T(8,128)(2,1)}) %all-gather.2.cloned.1.call-update) | async-done | bytes 2359312 | tf_op jit(solution)/shard_map/all_gather | solution.py:129
  592.5 92.8 %collective-permute-done.hx = bf16[32,2,20,16,128]{4,3,2,1,0:T(8,128)(2,1)} collective-permute-done((bf16[32,2,20,16,128]{4,3,2,1,0:T(8,128)(2,1)}, bf16[32,2,20,16,128]{4,3,2,1,0:T(8,128)(2,1)}, u32[]{:S(2)}, u32[]{:S(2)}) %collective-permute-start) | collective-permute-done | bytes 5242912 | tf_op jit(solution)/shard_map/ppermute | solution.py:128
  685.3 260.1 %shard_map.55 = f32[32,1024,512]{2,1,0:T(8,128)} custom-call(bf16[32,2,20,64,128]{4,3,2,1,0:T(8,128)(2,1)} %reshape.22.xg, bf16[32,2,20,16,128]{4,3,2,1,0:T(8,128)(2,1)} %collective-permute-done.hx, bf16[2304,512]{1,0:T(8,128)(2,1)} %bitcast.20, f32[1,512]{1,0:T(1,128)} %bitcast.21, bf16[4608,512]{1,0:T(8,128)(2,1)} %bitcast.19, f32[1,512]{1,0:T(1,128)} %bitcast.22), custom_call_target="tpu_custom_call" | custom-call | tf_op jit(solution)/shard_map/pallas_call | solution.py:99
Async XLA Ops:
  129.0 236.3 %all-to-all-start = ((bf16[4,2,1310720]{2,1,0:T(2,128)(2,1)}), bf16[4,2,1310720]{2,1,0:T(2,128)(2,1)}, u32[]{:S(2)}, u32[]{:S(2)}) async-start(bf16[4,2,1310720]{2,1,0:T(2,128)(2,1)} %reshape.28), calls=%async_computation | async-start | bytes 41943040 | tf_op jit(solution)/shard_map/all_to_all | solution.py:123
  136.7 455.8 %all-gather.2.cloned.1.call-start = ((), (), s32[]{:S(2)}) async-start(), calls=%async_computation.1 | async-start | bytes 2949120 | tf_op jit(solution)/shard_map/all_gather | solution.py:129
  570.1 115.2 %collective-permute-start = (bf16[32,2,20,16,128]{4,3,2,1,0:T(8,128)(2,1)}, bf16[32,2,20,16,128]{4,3,2,1,0:T(8,128)(2,1)}, u32[]{:S(2)}, u32[]{:S(2)}) collective-permute-start(bf16[32,2,20,16,128]{4,3,2,1,0:T(8,128)(2,1)} %slice_select_fusion), channel_id=1, source_target_pairs={{0,4},{4,0},{1,5},{5,1},{2,6},{6,2},{3,7},{7,3}} | collective-permute-start | bytes 15728648 | tf_op jit(solution)/shard_map/ppermute | solution.py:128
Sparse Core Ops, SparseCore 0:
  572.6 19.8 all-gather.1

commit v2 on v1

v2 whole, which is shorter than its diff:
```python
import functools

import jax
import jax.numpy as jnp
from jax import lax
from jax.experimental import pallas as pl
from jax.experimental.pallas import tpu as pltpu
from jax.sharding import PartitionSpec as P

ROWS = 16
COLS = 64
WIN = 20
MESH = pl.DeviceIdType.MESH
SLOT_A = 2
SLOT_S = 4
SLOT_X = 8
SLOT_H = 4


def shift_down(v, edge):
    rolled = pltpu.roll(v, 1, axis=0)
    pos = lax.broadcasted_iota(jnp.int32, v.shape, 0) % COLS
    return jnp.where(pos == 0, edge, rolled)


def shift_up(v, edge):
    rolled = pltpu.roll(v, v.shape[0] - 1, axis=0)
    pos = lax.broadcasted_iota(jnp.int32, v.shape, 0) % COLS
    return jnp.where(pos == COLS - 1, edge, rolled)


def build_x3(is_left, xc, hx, x3, xh):
    for half in range(2):
        lane = half * 128
        for r in range(WIN):
            mid = xc[half, 2 + r]
            v = mid.astype(jnp.float32)
            h = hx[half, r].astype(jnp.float32)
            near = jnp.where(is_left, h[0:1], h[15:16])
            far = jnp.where(is_left, h[1:2], h[14:15])
            own = jnp.where(is_left, v[COLS - 1:COLS], v[0:1])
            zero = jnp.zeros_like(near)
            rows = pl.ds(r * COLS, COLS)
            x3[rows, lane:lane + 128] = shift_down(v, jnp.where(is_left, zero, near)).astype(jnp.bfloat16)
            x3[rows, 256 + lane:384 + lane] = mid
            x3[rows, 512 + lane:640 + lane] = shift_up(v, jnp.where(is_left, near, zero)).astype(jnp.bfloat16)
            xh[r:r + 1, lane:lane + 128] = jnp.where(is_left, own, far)
            xh[r:r + 1, 256 + lane:384 + lane] = near
            xh[r:r + 1, 512 + lane:640 + lane] = jnp.where(is_left, far, own)


def conv1(is_left, top, bottom, x3, xh, w1, b1, y3, blocks=((0, 10), (10, 8))):
    edge_all = None
    for first, count in blocks:
        m = count * COLS
        lhs = jnp.concatenate([x3[(first + dy) * COLS:(first + dy) * COLS + m, :] for dy in range(3)], axis=1)
        if first == 0:
            edge = jnp.concatenate([xh[dy:dy + 32, :] for dy in range(3)], axis=1).astype(jnp.bfloat16)
            lhs = jnp.concatenate([edge, lhs], axis=0)
        z = jnp.dot(lhs, w1[...].reshape(2304, 512), preferred_element_type=jnp.float32)
        z = jnp.maximum(z + b1[...], 0.0)
        if first == 0:
            edge_all = z[:32]
            z = z[32:]
        for r in range(count):
            row = first + r
            v = z[r * COLS:(r + 1) * COLS]
            e = edge_all[row:row + 1]
            if row == 0:
                v = jnp.where(top, 0.0, v)
                e = jnp.where(top, 0.0, e)
            if row == ROWS + 1:
                v = jnp.where(bottom, 0.0, v)
                e = jnp.where(bottom, 0.0, e)
            zero = jnp.zeros_like(e)
            dst = pl.ds(row * COLS, COLS)
            y3[dst, 0:512] = shift_down(v, jnp.where(is_left, zero, e)).astype(jnp.bfloat16)
            y3[dst, 512:1024] = v.astype(jnp.bfloat16)
            y3[dst, 1024:1536] = shift_up(v, jnp.where(is_left, e, zero)).astype(jnp.bfloat16)


def conv2(y3, w2, b2, out, blk=8):
    for first in range(0, ROWS, blk):
        m = blk * COLS
        lhs = jnp.concatenate([y3[(first + dy) * COLS:(first + dy) * COLS + m, :] for dy in range(3)], axis=1)
        out[first * COLS:first * COLS + m, :] = jnp.dot(lhs, w2[...], preferred_element_type=jnp.float32) + b2[...]


def merge(slot, chip, off, ab, xc_slot, sb_slot):
    for r in range(WIN):
        xc_slot[chip, off + r] = jnp.concatenate([ab[slot, 0, 0, r], ab[slot, 0, 1, r]], axis=-1)
        sb_slot[r] = jnp.concatenate([ab[slot, 1, 0, r], ab[slot, 1, 1, r]], axis=-1)


def fused_kernel(images, x, w1, b1, w2, b2, y, ab, sb, xc, hx, x3, xh, y3, ob, w1v, w2v,
                 loc_sem, a_send, a_recv, x_send, x_recv, h_send, h_recv, o_sem, w_loc, w_send, w_recv,
                 credit_a, credit_x, credit_h):
    data = lax.axis_index('data')
    side = lax.axis_index('cols')
    model = lax.axis_index('model')
    is_left = side == 0
    chip = model // 2
    core = model % 2
    mate = chip * 2 + 1 - core
    far = (1 - chip) * 2 + core
    far_mate = (1 - chip) * 2 + 1 - core
    to_mate = (data, side, mate)
    to_far = (data, side, far)
    to_side = (data, 1 - side, model)

    def source(m):
        return jnp.where(m == 0, 0, jnp.where(m == 3, 44, ROWS * m - 2))

    def place(m):
        return jnp.where(m == 0, 4, jnp.where(m == 3, 0, 2))

    edge = pl.multiple_of(jnp.where(is_left, COLS - 16, 0), 16)

    for slot in range(SLOT_X):
        for half in range(2):
            for row in (2, 3, 20, 21):
                xc[slot, half, row] = jnp.zeros((COLS, 128), jnp.bfloat16)
    xh[...] = jnp.zeros_like(xh)

    barrier = pltpu.get_barrier_semaphore()
    for peer in (to_mate, to_far, to_side):
        pl.semaphore_signal(barrier, inc=1, device_id=peer, device_id_type=MESH)
    pl.semaphore_wait(barrier, 3)

    def remote(src, dst, send, recv, peer):
        return pltpu.make_async_remote_copy(src_ref=src, dst_ref=dst, send_sem=send, recv_sem=recv, device_id=peer, device_id_type=MESH)

    def w1_part(m):
        return w1v.at[:, pl.ds(pl.multiple_of(m * 64, 64), 64), :]

    w_far = remote(w1, w1_part(model), w_send.at[0], w_recv.at[0], to_far)
    w_mate = remote(w1, w1_part(model), w_send.at[1], w_recv.at[1], to_mate)
    w_pass = remote(w1_part(far), w1_part(far), w_send.at[2], w_recv.at[2], to_mate)
    w_own = pltpu.make_async_copy(w1, w1_part(model), w_loc.at[0])
    w2_own = pltpu.make_async_copy(w2, w2v, w_loc.at[1])

    def own_copy(n, win):
        slot = n % SLOT_A
        rows = pl.ds(source(model if win == 0 else far), WIN)
        return pltpu.make_async_copy(x.at[n, rows], ab.at[slot, win, core], loc_sem.at[slot, win])

    def mate_copy(n, win):
        slot = n % SLOT_A
        rows = pl.ds(source(mate if win == 0 else far_mate), WIN)
        return remote(x.at[n, rows], ab.at[slot, win, core], a_send.at[slot, win], a_recv.at[slot, win], to_mate)

    def far_copy(n):
        slot = n % SLOT_X
        return remote(sb.at[n % SLOT_S], xc.at[slot, chip, pl.ds(place(far), WIN)], x_send.at[slot], x_recv.at[slot], to_far)

    def far_land(n):
        slot = n % SLOT_X
        return remote(sb.at[n % SLOT_S], xc.at[slot, 1 - chip, pl.ds(place(model), WIN)], x_send.at[slot], x_recv.at[slot], to_far)

    def side_copy(n):
        slot = n % SLOT_H
        return remote(xc.at[n % SLOT_X, :, pl.ds(2, WIN), pl.ds(edge, 16), :], hx.at[slot], h_send.at[slot], h_recv.at[slot], to_side)

    def out_copy(n):
        return pltpu.make_async_copy(ob.at[n % 2], y.at[n], o_sem.at[n % 2])

    def within(n):
        return jnp.logical_and(n >= 0, n < images)

    def control(i):
        na, nm, nx, nh, nb = i + 6, i + 5, i + 4, i + 2, i + 1

        @pl.when(within(na))
        def _():
            @pl.when(na >= SLOT_A)
            def _():
                pl.semaphore_wait(credit_a, 1)
            for win in range(2):
                own_copy(na, win).start()
                mate_copy(na, win).start()

        @pl.when(within(nx))
        def _():
            @pl.when(nx >= SLOT_X)
            def _():
                pl.semaphore_wait(credit_x, 1)
            far_copy(nx).start()

        @pl.when(within(nm))
        def _():
            for win in range(2):
                own_copy(nm, win).wait()
                mate_copy(nm, win).wait()

        @pl.when(within(nh))
        def _():
            far_copy(nh).wait_send()
            far_land(nh).wait_recv()

            @pl.when(nh >= SLOT_H)
            def _():
                pl.semaphore_wait(credit_h, 1)
            side_copy(nh).start()

        @pl.when(within(nb))
        def _():
            side_copy(nb).wait()

    def release(i):
        nm, nb = i + 5, i + 1

        @pl.when(jnp.logical_and(nm >= 0, nm < images - SLOT_A))
        def _():
            pl.semaphore_signal(credit_a, inc=1, device_id=to_mate, device_id_type=MESH)

        @pl.when(jnp.logical_and(nb >= 0, nb < images - SLOT_X))
        def _():
            pl.semaphore_signal(credit_x, inc=1, device_id=to_far, device_id_type=MESH)

        @pl.when(jnp.logical_and(nb >= 0, nb < images - SLOT_H))
        def _():
            pl.semaphore_signal(credit_h, inc=1, device_id=to_side, device_id_type=MESH)

    def do_merge(n):
        merge(n % SLOT_A, chip, place(model), ab, xc.at[n % SLOT_X], sb.at[n % SLOT_S])

    def do_build(n):
        build_x3(is_left, xc.at[n % SLOT_X], hx.at[n % SLOT_H], x3, xh)

    w_far.start()
    w_mate.start()
    w_own.start()
    w2_own.start()

    def fill(t, _):
        i = t - 6
        control(i)

        @pl.when(within(i + 5))
        def _():
            do_merge(i + 5)

        @pl.when(within(i + 1))
        def _():
            do_build(i + 1)
        release(i)
        return 0

    lax.fori_loop(0, 6, fill, 0)
    w_far.wait()
    w_pass.start()
    w_mate.wait()
    w_own.wait()
    w2_own.wait()
    w_pass.wait()

    def step(i, _):
        control(i)

        @pl.when(i >= 2)
        def _():
            out_copy(i - 2).wait()
        conv1(is_left, model == 0, model == 3, x3, xh, w1v, b1, y3)
        do_build(jnp.minimum(i + 1, images - 1))
        do_merge(i + 5)
        conv2(y3, w2v, b2, ob.at[i % 2])
        out_copy(i).start()
        release(i)
        return 0

    lax.fori_loop(0, images, step, 0)
    out_copy(images - 2).wait()
    out_copy(images - 1).wait()


def fused(x, w1, b1, w2, b2):
    images = x.shape[0]
    hbm = pl.BlockSpec(memory_space=pl.ANY)
    vmem = pl.BlockSpec(memory_space=pltpu.VMEM)
    dma = pltpu.SemaphoreType.DMA
    bf16 = jnp.bfloat16
    return pl.pallas_call(
        functools.partial(fused_kernel, images),
        out_shape=jax.ShapeDtypeStruct((images, ROWS * COLS, 512), jnp.float32),
        in_specs=[hbm, hbm, vmem, hbm, vmem],
        out_specs=hbm,
        scratch_shapes=[
            pltpu.VMEM((SLOT_A, 2, 2, WIN, COLS, 64), bf16),
            pltpu.VMEM((SLOT_S, WIN, COLS, 128), bf16),
            pltpu.VMEM((SLOT_X, 2, WIN + 4, COLS, 128), bf16),
            pltpu.VMEM((SLOT_H, 2, WIN, 16, 128), bf16),
            pltpu.VMEM((WIN * COLS, 768), bf16),
            pltpu.VMEM((40, 768), jnp.float32),
            pltpu.VMEM(((ROWS + 2) * COLS, 1536), bf16),
            pltpu.VMEM((2, ROWS * COLS, 512), jnp.float32),
            pltpu.VMEM((9, 256, 512), bf16),
            pltpu.VMEM((4608, 512), bf16),
            dma((SLOT_A, 2)), dma((SLOT_A, 2)), dma((SLOT_A, 2)),
            dma((SLOT_X,)), dma((SLOT_X,)), dma((SLOT_H,)), dma((SLOT_H,)), dma((2,)),
            dma((2,)), dma((3,)), dma((3,)),
            pltpu.SemaphoreType.REGULAR, pltpu.SemaphoreType.REGULAR, pltpu.SemaphoreType.REGULAR,
        ],
        compiler_params=pltpu.CompilerParams(vmem_limit_bytes=60 * 1024 * 1024, collective_id=0, has_side_effects=True),
    )(x, w1, b1, w2, b2)


def solution(mesh):
    def local_step(x, w1, b1, w2, b2):
        images = x.shape[0]
        y = fused(x, w1.reshape(9, 64, 512), b1.reshape(1, 512), w2.reshape(4608, 512), b2.reshape(1, 512))
        return y.reshape(images, ROWS, COLS, 512)

    return jax.shard_map(local_step, mesh=mesh, in_specs=(P('data', None, 'cols', 'model'), P(None, None, 'model', None), P(), P(), P()), out_specs=P('data', 'model', 'cols', None), check_vma=False)
```

time: 954 us -> 347 us (0.36)
  waiting for transfers between devices: 341 us -> 0 us
  local copies, waits for them, and re-layouts: 292 us -> 43.6 us
  Pallas kernels: 260 us -> 303 us
  other arithmetic: 35.4 us -> 0 us
  between operations: 13.4 us -> 0.01 us
  starting transfers between devices: 10.3 us -> 0 us
    all_to_all x1 -> x0, waiting for transfers between devices: 228 us -> none  [local_step(): got = lax.all_to_all(tiles, 'model', 0, 0)]
    reshape x2 -> x0, local copies, waits for them, and re-layouts: 140 us -> none  [the longest x1 75.3 us: local_step(): got = got.reshape(2, 2, images, WIN, COLS, 64)]
    ppermute x1 -> x0, waiting for transfers between devices: 92.8 us -> none  [local_step(): hx = lax.ppermute(edge, 'cols', [(0, 1), (1, 0)])]
    unnamed x2 -> x1, local copies, waits for them, and re-layouts: 115 us -> 43.6 us
    pallas_call x1, Pallas kernels: 260 us -> 303 us  [fused(): pl.pallas_call(functools.partial(fused_kernel, images), out_shape=jax.Sha...]
    another operation x1 -> x0, local copies, waits for them, and re-layouts: 36.2 us -> none  [local_step(): tiles = jnp.stack([wide[:, ROWS * k:ROWS * k + WIN] for k in range(4)])]
    another operation x1 -> x0, other arithmetic: 28.4 us -> none  [local_step(): tiles = jnp.stack([wide[:, ROWS * k:ROWS * k + WIN] for k in range(4)])]
    all_gather x1 -> x0, waiting for transfers between devices: 20 us -> none  [local_step(): w1g = lax.all_gather(w1, 'model', axis=2, tiled=True).reshape(2304, 512)]
  transfers between devices with their start and end apart: 3 -> 0, of which waited for: 3 -> 0; matrix products, arithmetic and copies ran while one was open for 0% -> 0% of each run, Pallas kernels for 0% -> 0%
where the time goes in v2:
time: 347 us; the launch traced here: 346 us
  Pallas kernels  303 us (87%)
  local copies, waits for them, and re-layouts  43.6 us (13%)
    pallas_call x1, Pallas kernels, fused(): pl.pallas_call(functools.partial(fused_kernel, images), out_shape=jax.Sha...  303 us
    unnamed x1, local copies, waits for them, and re-layouts  43.6 us

profile of v2, /device:TPU:0, one launch (start us, length us, event | category | flops | bytes accessed | tf_op | source)
XLA Modules:
  0.0 346.5 jit_solution(9770013571737000186)
XLA Ops:
  0.0 302.8 %shard_map.55 = f32[32,1024,512]{2,1,0:T(8,128)} custom-call(bf16[32,64,64,64]{3,2,1,0:T(8,128)(2,1)} %x.1, bf16[9,64,512]{2,1,0:T(8,128)(2,1)} %bitcast.6, f32[1,512]{1,0:T(1,128)} %bitcast.7, bf16[4608,512]{1,0:T(8,128)(2,1)} %bitcast.5, f32[1,512]{1,0:T(1,128)} %bitcast.8), custom_call_target="tpu_custom_call" | custom-call | tf_op jit(solution)/shard_map/pallas_call | solution.py:282
  302.8 43.6 %copy.7 = f32[32,16,64,512]{3,2,1,0:T(8,128)} copy(f32[32,16,64,512]{3,2,1,0:T(8,128)} %bitcast.4) | data formatting | bytes 134217728

commit v3 on v2

--- a/solution.py
+++ b/solution.py
@@ -11,10 +11,11 @@
 COLS = 64
 WIN = 20
 MESH = pl.DeviceIdType.MESH
-SLOT_A = 2
-SLOT_S = 4
-SLOT_X = 8
-SLOT_H = 4
+SLOT_A = 4
+SLOT_S = 8
+SLOT_X = 16
+SLOT_H = 8
+LATER = 6
 
 
 def shift_down(v, edge):
@@ -92,9 +93,10 @@
         sb_slot[r] = jnp.concatenate([ab[slot, 1, 0, r], ab[slot, 1, 1, r]], axis=-1)
 
 
-def fused_kernel(images, x, w1, b1, w2, b2, y, ab, sb, xc, hx, x3, xh, y3, ob, w1v, w2v,
-                 loc_sem, a_send, a_recv, x_send, x_recv, h_send, h_recv, o_sem, w_loc, w_send, w_recv,
+def fused_kernel(images, x, w1, b1, w2, b2, y, x_rest, h_rest, w1_all, ab, sb, xc, hx, x3, xh, y3, ob, w1v, w2v,
+                 loc_sem, a_send, a_recv, x_send, x_recv, h_send, h_recv, o_sem, w_loc, w_send, w_recv, rest_sem,
                  credit_a, credit_x, credit_h):
+    now = images - LATER
     data = lax.axis_index('data')
     side = lax.axis_index('cols')
     model = lax.axis_index('model')
@@ -149,13 +151,22 @@
         rows = pl.ds(source(mate if win == 0 else far_mate), WIN)
         return remote(x.at[n, rows], ab.at[slot, win, core], a_send.at[slot, win], a_recv.at[slot, win], to_mate)
 
-    def far_copy(n):
+    def is_edge(m):
+        return jnp.logical_or(m == 0, m == 3)
+
+    def by_size(m, run):
+        @pl.when(is_edge(m))
+        def _():
+            run(WIN - 2, jnp.where(m == 3, 2, 0))
+
+        @pl.when(jnp.logical_not(is_edge(m)))
+        def _():
+            run(WIN, 0)
+
+    def far_copy(n, m, half, count, first):
         slot = n % SLOT_X
-        return remote(sb.at[n % SLOT_S], xc.at[slot, chip, pl.ds(place(far), WIN)], x_send.at[slot], x_recv.at[slot], to_far)
-
-    def far_land(n):
-        slot = n % SLOT_X
-        return remote(sb.at[n % SLOT_S], xc.at[slot, 1 - chip, pl.ds(place(model), WIN)], x_send.at[slot], x_recv.at[slot], to_far)
+        return remote(sb.at[n % SLOT_S, pl.ds(first, count)], xc.at[slot, half, pl.ds(place(m) + first, count)],
+                      x_send.at[slot], x_recv.at[slot], to_far)
 
     def side_copy(n):
         slot = n % SLOT_H
@@ -164,65 +175,90 @@
     def out_copy(n):
         return pltpu.make_async_copy(ob.at[n % 2], y.at[n], o_sem.at[n % 2])
 
-    def within(n):
-        return jnp.logical_and(n >= 0, n < images)
+    def rest_copy(n, part):
+        if part == 0:
+            return pltpu.make_async_copy(xc.at[n % SLOT_X, :, pl.ds(2, WIN)], x_rest.at[n - now], rest_sem.at[n - now, 0])
+        return pltpu.make_async_copy(hx.at[n % SLOT_H], h_rest.at[n - now], rest_sem.at[n - now, 1])
+
+    def last(i):
+        return jnp.clip(i + 6 + jnp.maximum(i, 0) // 4, -1, images - 1)
+
+    def each(i, run):
+        lo, hi = last(i - 1), last(i)
+
+        @pl.when(hi > lo)
+        def _():
+            run(lo + 1)
+
+        @pl.when(hi > lo + 1)
+        def _():
+            run(lo + 2)
+
+    def start_a(n):
+        @pl.when(n >= SLOT_A)
+        def _():
+            pl.semaphore_wait(credit_a, 1)
+        for win in range(2):
+            own_copy(n, win).start()
+            mate_copy(n, win).start()
+
+    def start_x(n):
+        @pl.when(n >= SLOT_X)
+        def _():
+            pl.semaphore_wait(credit_x, 1)
+        by_size(far, lambda count, first: far_copy(n, far, chip, count, first).start())
+
+    def wait_a(n):
+        for win in range(2):
+            own_copy(n, win).wait()
+            mate_copy(n, win).wait()
+
+    def start_h(n):
+        by_size(far, lambda count, first: far_copy(n, far, chip, count, first).wait_send())
+        by_size(model, lambda count, first: far_copy(n, model, 1 - chip, count, first).wait_recv())
+
+        @pl.when(n >= SLOT_H)
+        def _():
+            pl.semaphore_wait(credit_h, 1)
+        side_copy(n).start()
+
+    def wait_h(n):
+        side_copy(n).wait()
+
+        @pl.when(n >= now)
+        def _():
+            rest_copy(n, 0).start()
+            rest_copy(n, 1).start()
 
     def control(i):
-        na, nm, nx, nh, nb = i + 6, i + 5, i + 4, i + 2, i + 1
-
-        @pl.when(within(na))
-        def _():
-            @pl.when(na >= SLOT_A)
+        each(i, start_a)
+        each(i - 2, start_x)
+        each(i - 1, wait_a)
+
+        @pl.when(last(i - 1) > last(i - 2) + 1)
+        def _():
+            do_merge(last(i - 1) - 1, True)
+        each(i - 4, start_h)
+        each(i - 5, wait_h)
+
+    def release(i):
+        def free_a(n):
+            @pl.when(n < images - SLOT_A)
             def _():
-                pl.semaphore_wait(credit_a, 1)
-            for win in range(2):
-                own_copy(na, win).start()
-                mate_copy(na, win).start()
-
-        @pl.when(within(nx))
-        def _():
-            @pl.when(nx >= SLOT_X)
-            def _():
-                pl.semaphore_wait(credit_x, 1)
-            far_copy(nx).start()
-
-        @pl.when(within(nm))
-        def _():
-            for win in range(2):
-                own_copy(nm, win).wait()
-                mate_copy(nm, win).wait()
-
-        @pl.when(within(nh))
-        def _():
-            far_copy(nh).wait_send()
-            far_land(nh).wait_recv()
-
-            @pl.when(nh >= SLOT_H)
-            def _():
-                pl.semaphore_wait(credit_h, 1)
-            side_copy(nh).start()
-
-        @pl.when(within(nb))
-        def _():
-            side_copy(nb).wait()
-
-    def release(i):
-        nm, nb = i + 5, i + 1
-
-        @pl.when(jnp.logical_and(nm >= 0, nm < images - SLOT_A))
-        def _():
-            pl.semaphore_signal(credit_a, inc=1, device_id=to_mate, device_id_type=MESH)
-
-        @pl.when(jnp.logical_and(nb >= 0, nb < images - SLOT_X))
+                pl.semaphore_signal(credit_a, inc=1, device_id=to_mate, device_id_type=MESH)
+        each(i - 1, free_a)
+        built = i + 1
+
+        @pl.when(jnp.logical_and(built >= 0, built < images - SLOT_X))
         def _():
             pl.semaphore_signal(credit_x, inc=1, device_id=to_far, device_id_type=MESH)
 
-        @pl.when(jnp.logical_and(nb >= 0, nb < images - SLOT_H))
+        @pl.when(jnp.logical_and(built >= 0, built < images - SLOT_H))
         def _():
             pl.semaphore_signal(credit_h, inc=1, device_id=to_side, device_id_type=MESH)
 
-    def do_merge(n):
-        merge(n % SLOT_A, chip, place(model), ab, xc.at[n % SLOT_X], sb.at[n % SLOT_S])
+    def do_merge(n, live):
+        merge(n % SLOT_A, chip, place(model), ab, xc.at[jnp.where(live, n % SLOT_X, SLOT_X)], sb.at[jnp.where(live, n % SLOT_S, SLOT_S)])
 
     def do_build(n):
         build_x3(is_left, xc.at[n % SLOT_X], hx.at[n % SLOT_H], x3, xh)
@@ -236,11 +272,11 @@
         i = t - 6
         control(i)
 
-        @pl.when(within(i + 5))
-        def _():
-            do_merge(i + 5)
-
-        @pl.when(within(i + 1))
+        @pl.when(last(i - 1) > last(i - 2))
+        def _():
+            do_merge(last(i - 1), True)
+
+        @pl.when(i + 1 >= 0)
         def _():
             do_build(i + 1)
         release(i)
@@ -253,6 +289,8 @@
     w_own.wait()
     w2_own.wait()
     w_pass.wait()
+    w_out = pltpu.make_async_copy(w1v, w1_all, w_loc.at[2])
+    w_out.start()
 
     def step(i, _):
         control(i)
@@ -261,16 +299,106 @@
         def _():
             out_copy(i - 2).wait()
         conv1(is_left, model == 0, model == 3, x3, xh, w1v, b1, y3)
-        do_build(jnp.minimum(i + 1, images - 1))
-        do_merge(i + 5)
+        do_build(i + 1)
+        do_merge(last(i - 1), last(i - 1) > last(i - 2))
         conv2(y3, w2v, b2, ob.at[i % 2])
         out_copy(i).start()
         release(i)
         return 0
 
-    lax.fori_loop(0, images, step, 0)
-    out_copy(images - 2).wait()
-    out_copy(images - 1).wait()
+    lax.fori_loop(0, now, step, 0)
+    out_copy(now - 2).wait()
+    out_copy(now - 1).wait()
+    w_out.wait()
+    for n in range(now, images):
+        rest_copy(n, 0).wait()
+        rest_copy(n, 1).wait()
+
+
+def rest_kernel(images, y_done, x_rest, h_rest, w1, b1, w2, b2, y, xc, hx, x3, xh, y3, ob, w1v, w2v, cb,
+                l_sem, w_sem, o_sem, in_sem, out_sem):
+    done = images - LATER
+    sets = LATER - 1
+    size = -(-done // sets)
+    model = lax.axis_index('model')
+    is_left = lax.axis_index('cols') == 0
+    weights = [pltpu.make_async_copy(w1, w1v, w_sem.at[0]), pltpu.make_async_copy(w2, w2v, w_sem.at[1])]
+    xh[...] = jnp.zeros_like(xh)
+
+    def load(n):
+        return [pltpu.make_async_copy(x_rest.at[n], xc.at[n, :, pl.ds(2, WIN)], l_sem.at[n, 0]),
+                pltpu.make_async_copy(h_rest.at[n], hx.at[n], l_sem.at[n, 1])]
+
+    def bring(s, q):
+        return pltpu.make_async_copy(y_done.at[s + sets * q], cb.at[s % 2, q], in_sem.at[s % 2, q])
+
+    def put(s, q):
+        return pltpu.make_async_copy(cb.at[s % 2, q], y.at[s + sets * q], out_sem.at[s % 2, q])
+
+    def each(s, run):
+        for q in range(size):
+            @pl.when(jnp.logical_and(jnp.logical_and(s >= 0, s < sets), s + sets * q < done))
+            def _():
+                run(s, q)
+
+    def out_copy(n):
+        return pltpu.make_async_copy(ob.at[n % 2], y.at[done + n], o_sem.at[n % 2])
+
+    for copy in load(0) + weights[:1] + load(1) + weights[1:] + [c for n in range(2, LATER) for c in load(n)]:
+        copy.start()
+    for copy in load(0):
+        copy.wait()
+    build_x3(is_left, xc.at[0], hx.at[0], x3, xh)
+    for copy in weights + [c for n in range(1, LATER) for c in load(n)]:
+        copy.wait()
+
+    def step(i, _):
+        each(i - 1, lambda s, q: bring(s, q).wait())
+        each(i - 1, lambda s, q: put(s, q).start())
+        each(i - 2, lambda s, q: put(s, q).wait())
+        each(i, lambda s, q: bring(s, q).start())
+
+        @pl.when(i >= 2)
+        def _():
+            out_copy(i - 2).wait()
+        conv1(is_left, model == 0, model == 3, x3, xh, w1v, b1, y3)
+        n = jnp.minimum(i + 1, LATER - 1)
+        build_x3(is_left, xc.at[n], hx.at[n], x3, xh)
+        conv2(y3, w2v, b2, ob.at[i % 2])
+        out_copy(i).start()
+        return 0
+
+    lax.fori_loop(0, LATER, step, 0)
+    each(jnp.int32(sets - 1), lambda s, q: put(s, q).wait())
+    out_copy(LATER - 2).wait()
+    out_copy(LATER - 1).wait()
+
+
+def rest(images, y_done, x_rest, h_rest, w1, b1, w2, b2):
+    hbm = pl.BlockSpec(memory_space=pl.ANY)
+    vmem = pl.BlockSpec(memory_space=pltpu.VMEM)
+    dma = pltpu.SemaphoreType.DMA
+    bf16 = jnp.bfloat16
+    size = -(-(images - LATER) // (LATER - 1))
+    return pl.pallas_call(
+        functools.partial(rest_kernel, images),
+        out_shape=jax.ShapeDtypeStruct((images, ROWS * COLS, 512), jnp.float32),
+        in_specs=[hbm, hbm, hbm, hbm, vmem, hbm, vmem],
+        out_specs=hbm,
+        scratch_shapes=[
+            pltpu.VMEM((LATER, 2, WIN + 4, COLS, 128), bf16),
+            pltpu.VMEM((LATER, 2, WIN, 16, 128), bf16),
+            pltpu.VMEM((WIN * COLS, 768), bf16),
+            pltpu.VMEM((40, 768), jnp.float32),
+            pltpu.VMEM(((ROWS + 2) * COLS, 1536), bf16),
+            pltpu.VMEM((2, ROWS * COLS, 512), jnp.float32),
+            pltpu.VMEM((9, 256, 512), bf16),
+            pltpu.VMEM((4608, 512), bf16),
+            pltpu.VMEM((2, size, ROWS * COLS, 512), jnp.float32),
+            dma((LATER, 2)), dma((2,)), dma((2,)), dma((2, size)), dma((2, size)),
+        ],
+        compiler_params=pltpu.CompilerParams(vmem_limit_bytes=62 * 1024 * 1024),
+    )(y_done, x_rest, h_rest, w1, b1, w2, b2)
 
 
 def fused(x, w1, b1, w2, b2):
@@ -281,13 +409,18 @@
     bf16 = jnp.bfloat16
     return pl.pallas_call(
         functools.partial(fused_kernel, images),
-        out_shape=jax.ShapeDtypeStruct((images, ROWS * COLS, 512), jnp.float32),
+        out_shape=[
+            jax.ShapeDtypeStruct((images - LATER, ROWS * COLS, 512), jnp.float32),
+            jax.ShapeDtypeStruct((LATER, 2, WIN, COLS, 128), bf16),
+            jax.ShapeDtypeStruct((LATER, 2, WIN, 16, 128), bf16),
+            jax.ShapeDtypeStruct((9, 256, 512), bf16),
+        ],
         in_specs=[hbm, hbm, vmem, hbm, vmem],
-        out_specs=hbm,
+        out_specs=[hbm] * 4,
         scratch_shapes=[
             pltpu.VMEM((SLOT_A, 2, 2, WIN, COLS, 64), bf16),
-            pltpu.VMEM((SLOT_S, WIN, COLS, 128), bf16),
-            pltpu.VMEM((SLOT_X, 2, WIN + 4, COLS, 128), bf16),
+            pltpu.VMEM((SLOT_S + 1, WIN, COLS, 128), bf16),
+            pltpu.VMEM((SLOT_X + 1, 2, WIN + 4, COLS, 128), bf16),
             pltpu.VMEM((SLOT_H, 2, WIN, 16, 128), bf16),
             pltpu.VMEM((WIN * COLS, 768), bf16),
             pltpu.VMEM((40, 768), jnp.float32),
@@ -297,7 +430,7 @@
             pltpu.VMEM((4608, 512), bf16),
             dma((SLOT_A, 2)), dma((SLOT_A, 2)), dma((SLOT_A, 2)),
             dma((SLOT_X,)), dma((SLOT_X,)), dma((SLOT_H,)), dma((SLOT_H,)), dma((2,)),
-            dma((2,)), dma((3,)), dma((3,)),
+            dma((3,)), dma((3,)), dma((3,)), dma((LATER, 2)),
             pltpu.SemaphoreType.REGULAR, pltpu.SemaphoreType.REGULAR, pltpu.SemaphoreType.REGULAR,
         ],
         compiler_params=pltpu.CompilerParams(vmem_limit_bytes=60 * 1024 * 1024, collective_id=0, has_side_effects=True),
@@ -307,7 +440,9 @@
 def solution(mesh):
     def local_step(x, w1, b1, w2, b2):
         images = x.shape[0]
-        y = fused(x, w1.reshape(9, 64, 512), b1.reshape(1, 512), w2.reshape(4608, 512), b2.reshape(1, 512))
+        b1, w2, b2 = b1.reshape(1, 512), w2.reshape(4608, 512), b2.reshape(1, 512)
+        done, x_rest, h_rest, w1_all = fused(x, w1.reshape(9, 64, 512), b1, w2, b2)
+        y = rest(images, done, x_rest, h_rest, w1_all, b1, w2, b2)
         return y.reshape(images, ROWS, COLS, 512)
 
     return jax.shard_map(local_step, mesh=mesh, in_specs=(P('data', None, 'cols', 'model'), P(None, None, 'model', None), P(), P(), P()), out_specs=P('data', 'model', 'cols', None), check_vma=False)

time: 347 us -> 312 us (0.90)
  local copies, waits for them, and re-layouts: 43.6 us -> 0 us
  Pallas kernels: 303 us -> 311 us
    unnamed x1 -> x0, local copies, waits for them, and re-layouts: 43.6 us -> none
    pallas_call x1 -> x2, Pallas kernels: 303 us -> 311 us  [the longest x1 255 us: fused(): pl.pallas_call(functools.partial(fused_kernel, images), out_shape=[jax.Sh...]
where the time goes in v3:
time: 312 us; the launch traced here: 311 us
  Pallas kernels  311 us (100%)
    pallas_call x1, Pallas kernels, fused(): pl.pallas_call(functools.partial(fused_kernel, images), out_shape=[jax.Sh...  255 us
    pallas_call x1, Pallas kernels, rest(): pl.pallas_call(functools.partial(rest_kernel, images), out_shape=jax.Shap...  56.4 us

profile of v3, /device:TPU:0, one launch (start us, length us, event | category | flops | bytes accessed | tf_op | source)
XLA Modules:
  0.0 311.5 jit_solution(3289956803014055371)
XLA Ops:
  0.0 254.9 %shard_map.55 = (f32[26,1024,512]{2,1,0:T(8,128)}, bf16[6,2,20,64,128]{4,3,2,1,0:T(8,128)(2,1)}, bf16[6,2,20,16,128]{4,3,2,1,0:T(8,128)(2,1)}, bf16[9,256,512]{2,1,0:T(8,128)(2,1)}) custom-call(bf16[32,64,64,64]{3,2,1,0:T(8,128)(2,1)} %x.1, bf16[9,64,512]{2,1,0:T(8,128)(2,1)} %bitcast.7, f32[1,512]{1,0:T(1,128)} %bitcast.8, bf16[4608,512]{1,0:T(8,128)(2,1)} %bitcast.5, ...), custom_call_target="tpu_custom_call" | custom-call | tf_op jit(solution)/shard_map/pallas_call | solution.py:410
  254.9 56.4 %shard_map.56 = f32[32,1024,512]{2,1,0:T(8,128)} custom-call(f32[26,1024,512]{2,1,0:T(8,128)} %get-tuple-element.9.y_done, bf16[6,2,20,64,128]{4,3,2,1,0:T(8,128)(2,1)} %get-tuple-element.10.x_rest, bf16[6,2,20,16,128]{4,3,2,1,0:T(8,128)(2,1)} %get-tuple-element.11.h_rest, bf16[9,256,512]{2,1,0:T(8,128)(2,1)} %get-tuple-element.12.w1, f32[1,512]{1,0:T(1,128)} %bitcast.9, ...), custom_call_target="tpu_custom_call" | custom-call | tf_op jit(solution)/shard_map/pallas_call | solution.py:383

commit v4 on v3

--- a/solution.py
+++ b/solution.py
@@ -10,6 +10,7 @@
 ROWS = 16
 COLS = 64
 WIN = 20
+EDGE = 8
 MESH = pl.DeviceIdType.MESH
 SLOT_A = 4
 SLOT_S = 8
@@ -37,8 +38,8 @@
             mid = xc[half, 2 + r]
             v = mid.astype(jnp.float32)
             h = hx[half, r].astype(jnp.float32)
-            near = jnp.where(is_left, h[0:1], h[15:16])
-            far = jnp.where(is_left, h[1:2], h[14:15])
+            near = jnp.where(is_left, h[0:1], h[EDGE - 1:EDGE])
+            far = jnp.where(is_left, h[1:2], h[EDGE - 2:EDGE - 1])
             own = jnp.where(is_left, v[COLS - 1:COLS], v[0:1])
             zero = jnp.zeros_like(near)
             rows = pl.ds(r * COLS, COLS)
@@ -116,7 +117,7 @@
     def place(m):
         return jnp.where(m == 0, 4, jnp.where(m == 3, 0, 2))
 
-    edge = pl.multiple_of(jnp.where(is_left, COLS - 16, 0), 16)
+    edge = pl.multiple_of(jnp.where(is_left, COLS - EDGE, 0), EDGE)
 
     for slot in range(SLOT_X):
         for half in range(2):
@@ -135,9 +136,14 @@
     def w1_part(m):
         return w1v.at[:, pl.ds(pl.multiple_of(m * 64, 64), 64), :]
 
-    w_far = remote(w1, w1_part(model), w_send.at[0], w_recv.at[0], to_far)
+    def w1_half(m, half):
+        return w1v.at[:, pl.ds(pl.multiple_of(m * 64, 64), 64), pl.ds(pl.multiple_of(half * 256, 256), 256)]
+
+    w_far = remote(w1.at[:, :, pl.ds(pl.multiple_of(side * 256, 256), 256)], w1_half(model, side), w_send.at[0], w_recv.at[0], to_far)
+    w_side = remote(w1_half(far, side), w1_half(far, side), w_send.at[3], w_recv.at[3], to_side)
+    w_pass = [remote(w1_half(far, half), w1_half(far, half), w_send.at[2 + 2 * t], w_recv.at[2 + 2 * t], to_mate)
+              for t, half in enumerate((side, 1 - side))]
     w_mate = remote(w1, w1_part(model), w_send.at[1], w_recv.at[1], to_mate)
-    w_pass = remote(w1_part(far), w1_part(far), w_send.at[2], w_recv.at[2], to_mate)
     w_own = pltpu.make_async_copy(w1, w1_part(model), w_loc.at[0])
     w2_own = pltpu.make_async_copy(w2, w2v, w_loc.at[1])
 
@@ -170,7 +176,7 @@
 
     def side_copy(n):
         slot = n % SLOT_H
-        return remote(xc.at[n % SLOT_X, :, pl.ds(2, WIN), pl.ds(edge, 16), :], hx.at[slot], h_send.at[slot], h_recv.at[slot], to_side)
+        return remote(xc.at[n % SLOT_X, :, pl.ds(2, WIN), pl.ds(edge, EDGE), :], hx.at[slot], h_send.at[slot], h_recv.at[slot], to_side)
 
     def out_copy(n):
         return pltpu.make_async_copy(ob.at[n % 2], y.at[n], o_sem.at[n % 2])
@@ -270,6 +276,17 @@
 
     def fill(t, _):
         i = t - 6
+
+        @pl.when(i == -2)
+        def _():
+            w_far.wait()
+            w_side.start()
+            w_pass[0].start()
+
+        @pl.when(i == -1)
+        def _():
+            w_side.wait()
+            w_pass[1].start()
         control(i)
 
         @pl.when(last(i - 1) > last(i - 2))
@@ -283,12 +300,11 @@
         return 0
 
     lax.fori_loop(0, 6, fill, 0)
-    w_far.wait()
-    w_pass.start()
     w_mate.wait()
     w_own.wait()
     w2_own.wait()
-    w_pass.wait()
+    for copy in w_pass:
+        copy.wait()
     w_out = pltpu.make_async_copy(w1v, w1_all, w_loc.at[2])
     w_out.start()
 
@@ -387,7 +403,7 @@
         out_specs=hbm,
         scratch_shapes=[
             pltpu.VMEM((LATER, 2, WIN + 4, COLS, 128), bf16),
-            pltpu.VMEM((LATER, 2, WIN, 16, 128), bf16),
+            pltpu.VMEM((LATER, 2, WIN, EDGE, 128), bf16),
             pltpu.VMEM((WIN * COLS, 768), bf16),
             pltpu.VMEM((40, 768), jnp.float32),
             pltpu.VMEM(((ROWS + 2) * COLS, 1536), bf16),
@@ -412,7 +428,7 @@
         out_shape=[
             jax.ShapeDtypeStruct((images - LATER, ROWS * COLS, 512), jnp.float32),
             jax.ShapeDtypeStruct((LATER, 2, WIN, COLS, 128), bf16),
-            jax.ShapeDtypeStruct((LATER, 2, WIN, 16, 128), bf16),
+            jax.ShapeDtypeStruct((LATER, 2, WIN, EDGE, 128), bf16),
             jax.ShapeDtypeStruct((9, 256, 512), bf16),
         ],
         in_specs=[hbm, hbm, vmem, hbm, vmem],
@@ -421,7 +437,7 @@
             pltpu.VMEM((SLOT_A, 2, 2, WIN, COLS, 64), bf16),
             pltpu.VMEM((SLOT_S + 1, WIN, COLS, 128), bf16),
             pltpu.VMEM((SLOT_X + 1, 2, WIN + 4, COLS, 128), bf16),
-            pltpu.VMEM((SLOT_H, 2, WIN, 16, 128), bf16),
+            pltpu.VMEM((SLOT_H, 2, WIN, EDGE, 128), bf16),
             pltpu.VMEM((WIN * COLS, 768), bf16),
             pltpu.VMEM((40, 768), jnp.float32),
             pltpu.VMEM(((ROWS + 2) * COLS, 1536), bf16),
@@ -430,7 +446,7 @@
             pltpu.VMEM((4608, 512), bf16),
             dma((SLOT_A, 2)), dma((SLOT_A, 2)), dma((SLOT_A, 2)),
             dma((SLOT_X,)), dma((SLOT_X,)), dma((SLOT_H,)), dma((SLOT_H,)), dma((2,)),
-            dma((3,)), dma((3,)), dma((3,)), dma((LATER, 2)),
+            dma((3,)), dma((5,)), dma((5,)), dma((LATER, 2)),
             pltpu.SemaphoreType.REGULAR, pltpu.SemaphoreType.REGULAR, pltpu.SemaphoreType.REGULAR,
         ],
         compiler_params=pltpu.CompilerParams(vmem_limit_bytes=60 * 1024 * 1024, collective_id=0, has_side_effects=True),

time: 312 us -> 305 us (0.978)
  Pallas kernels: 311 us -> 305 us
    pallas_call x1, Pallas kernels: 255 us -> 249 us  [fused(): pl.pallas_call(functools.partial(fused_kernel, images), out_shape=[jax.Sh...]
where the time goes in v4:
time: 305 us
  Pallas kernels  305 us (100%)
    pallas_call x1, Pallas kernels, fused(): pl.pallas_call(functools.partial(fused_kernel, images), out_shape=[jax.Sh...  249 us
    pallas_call x1, Pallas kernels, rest(): pl.pallas_call(functools.partial(rest_kernel, images), out_shape=jax.Shap...  56.3 us

profile of v4, /device:TPU:0, one launch (start us, length us, event | category | flops | bytes accessed | tf_op | source)
XLA Modules:
  0.0 305.1 jit_solution(6994115972899719841)
XLA Ops:
  0.0 248.6 %shard_map.55 = (f32[26,1024,512]{2,1,0:T(8,128)}, bf16[6,2,20,64,128]{4,3,2,1,0:T(8,128)(2,1)}, bf16[6,2,20,8,128]{4,3,2,1,0:T(8,128)(2,1)}, bf16[9,256,512]{2,1,0:T(8,128)(2,1)}) custom-call(bf16[32,64,64,64]{3,2,1,0:T(8,128)(2,1)} %x.1, bf16[9,64,512]{2,1,0:T(8,128)(2,1)} %bitcast.7, f32[1,512]{1,0:T(1,128)} %bitcast.8, bf16[4608,512]{1,0:T(8,128)(2,1)} %bitcast.5, ...), custom_call_target="tpu_custom_call" | custom-call | tf_op jit(solution)/shard_map/pallas_call | solution.py:426
  248.6 56.3 %shard_map.56 = f32[32,1024,512]{2,1,0:T(8,128)} custom-call(f32[26,1024,512]{2,1,0:T(8,128)} %get-tuple-element.9.y_done, bf16[6,2,20,64,128]{4,3,2,1,0:T(8,128)(2,1)} %get-tuple-element.10.x_rest, bf16[6,2,20,8,128]{4,3,2,1,0:T(8,128)(2,1)} %get-tuple-element.11.h_rest, bf16[9,256,512]{2,1,0:T(8,128)(2,1)} %get-tuple-element.12.w1, f32[1,512]{1,0:T(1,128)} %bitcast.9, ...), custom_call_target="tpu_custom_call" | custom-call | tf_op jit(solution)/shard_map/pallas_call | solution.py:399

commit v5 on v4

--- a/solution.py
+++ b/solution.py
@@ -13,10 +13,12 @@
 EDGE = 8
 MESH = pl.DeviceIdType.MESH
 SLOT_A = 4
-SLOT_S = 8
-SLOT_X = 16
+SLOT_S = 10
+SLOT_X = 12
 SLOT_H = 8
 LATER = 6
+EARLY = 10
+HALO = 32
 
 
 def shift_down(v, edge):
@@ -31,39 +33,62 @@
     return jnp.where(pos == COLS - 1, edge, rolled)
 
 
+def build_half(is_left, xc, hx, x3, xh):
+    for r in range(WIN):
+        mid = xc[2 + r]
+        v = mid.astype(jnp.float32)
+        h = hx[r].astype(jnp.float32)
+        near = jnp.where(is_left, h[0:1], h[EDGE - 1:EDGE])
+        far = jnp.where(is_left, h[1:2], h[EDGE - 2:EDGE - 1])
+        own = jnp.where(is_left, v[COLS - 1:COLS], v[0:1])
+        zero = jnp.zeros_like(near)
+        rows = pl.ds(r * COLS, COLS)
+        x3[rows, 0:128] = shift_down(v, jnp.where(is_left, zero, near)).astype(jnp.bfloat16)
+        x3[rows, 128:256] = mid
+        x3[rows, 256:384] = shift_up(v, jnp.where(is_left, near, zero)).astype(jnp.bfloat16)
+        xh[r:r + 1, 0:128] = jnp.where(is_left, own, far)
+        xh[r:r + 1, 128:256] = near
+        xh[r:r + 1, 256:384] = jnp.where(is_left, far, own)
+
+
 def build_x3(is_left, xc, hx, x3, xh):
     for half in range(2):
-        lane = half * 128
-        for r in range(WIN):
-            mid = xc[half, 2 + r]
-            v = mid.astype(jnp.float32)
-            h = hx[half, r].astype(jnp.float32)
-            near = jnp.where(is_left, h[0:1], h[EDGE - 1:EDGE])
-            far = jnp.where(is_left, h[1:2], h[EDGE - 2:EDGE - 1])
-            own = jnp.where(is_left, v[COLS - 1:COLS], v[0:1])
-            zero = jnp.zeros_like(near)
-            rows = pl.ds(r * COLS, COLS)
-            x3[rows, lane:lane + 128] = shift_down(v, jnp.where(is_left, zero, near)).astype(jnp.bfloat16)
-            x3[rows, 256 + lane:384 + lane] = mid
-            x3[rows, 512 + lane:640 + lane] = shift_up(v, jnp.where(is_left, near, zero)).astype(jnp.bfloat16)
-            xh[r:r + 1, lane:lane + 128] = jnp.where(is_left, own, far)
-            xh[r:r + 1, 256 + lane:384 + lane] = near
-            xh[r:r + 1, 512 + lane:640 + lane] = jnp.where(is_left, far, own)
-
-
-def conv1(is_left, top, bottom, x3, xh, w1, b1, y3, blocks=((0, 10), (10, 8))):
+        build_half(is_left, xc.at[half], hx.at[half], x3.at[half], xh.at[half])
+
+
+BLOCKS = ((0, 10), (10, 8))
+
+
+def lhs_rows(x3s, xhs, first, count):
+    m = count * COLS
+    lhs = jnp.concatenate([x3[(first + dy) * COLS:(first + dy) * COLS + m, :] for x3 in x3s for dy in range(3)], axis=1)
+    if first == 0:
+        edge = jnp.concatenate([xh[dy:dy + HALO, :] for xh in xhs for dy in range(3)], axis=1).astype(jnp.bfloat16)
+        lhs = jnp.concatenate([edge, lhs], axis=0)
+    return lhs
+
+
+def part_rows(first, count):
+    start = 0 if first == 0 else HALO + first * COLS
+    return slice(start, HALO + (first + count) * COLS)
+
+
+def conv1_part(x3, xh, w, zp):
+    for first, count in BLOCKS:
+        z = jnp.dot(lhs_rows([x3], [xh], first, count), w[...].reshape(1152, 512), preferred_element_type=jnp.float32)
+        zp[part_rows(first, count), :] = z.astype(jnp.bfloat16)
+
+
+def conv1(is_left, top, bottom, x3s, xhs, w, depth, b1, y3, zp=None):
     edge_all = None
-    for first, count in blocks:
-        m = count * COLS
-        lhs = jnp.concatenate([x3[(first + dy) * COLS:(first + dy) * COLS + m, :] for dy in range(3)], axis=1)
-        if first == 0:
-            edge = jnp.concatenate([xh[dy:dy + 32, :] for dy in range(3)], axis=1).astype(jnp.bfloat16)
-            lhs = jnp.concatenate([edge, lhs], axis=0)
-        z = jnp.dot(lhs, w1[...].reshape(2304, 512), preferred_element_type=jnp.float32)
+    for first, count in BLOCKS:
+        z = jnp.dot(lhs_rows(x3s, xhs, first, count), w[...].reshape(depth, 512), preferred_element_type=jnp.float32)
+        if zp is not None:
+            z = z + zp[part_rows(first, count), :].astype(jnp.float32)
         z = jnp.maximum(z + b1[...], 0.0)
         if first == 0:
-            edge_all = z[:32]
-            z = z[32:]
+            edge_all = z[:HALO]
+            z = z[HALO:]
         for r in range(count):
             row = first + r
             v = z[r * COLS:(r + 1) * COLS]
@@ -94,8 +119,8 @@
         sb_slot[r] = jnp.concatenate([ab[slot, 1, 0, r], ab[slot, 1, 1, r]], axis=-1)
 
 
-def fused_kernel(images, x, w1, b1, w2, b2, y, x_rest, h_rest, w1_all, ab, sb, xc, hx, x3, xh, y3, ob, w1v, w2v,
-                 loc_sem, a_send, a_recv, x_send, x_recv, h_send, h_recv, o_sem, w_loc, w_send, w_recv, rest_sem,
+def fused_kernel(images, x, w1, b1, w2, b2, y, x_rest, h_rest, w1_all, ab, sb, xc, hx, x3, xh, y3, ob, w1v, w2v, hp, zp,
+                 loc_sem, a_send, a_recv, x_send, x_recv, h_send, h_recv, o_sem, w_loc, w_send, w_recv, rest_sem, p_send, p_recv,
                  credit_a, credit_x, credit_h):
     now = images - LATER
     data = lax.axis_index('data')
@@ -134,10 +159,10 @@
         return pltpu.make_async_remote_copy(src_ref=src, dst_ref=dst, send_sem=send, recv_sem=recv, device_id=peer, device_id_type=MESH)
 
     def w1_part(m):
-        return w1v.at[:, pl.ds(pl.multiple_of(m * 64, 64), 64), :]
+        return w1v.at[m // 2, :, pl.ds(pl.multiple_of(m % 2 * 64, 64), 64), :]
 
     def w1_half(m, half):
-        return w1v.at[:, pl.ds(pl.multiple_of(m * 64, 64), 64), pl.ds(pl.multiple_of(half * 256, 256), 256)]
+        return w1v.at[m // 2, :, pl.ds(pl.multiple_of(m % 2 * 64, 64), 64), pl.ds(pl.multiple_of(half * 256, 256), 256)]
 
     w_far = remote(w1.at[:, :, pl.ds(pl.multiple_of(side * 256, 256), 256)], w1_half(model, side), w_send.at[0], w_recv.at[0], to_far)
     w_side = remote(w1_half(far, side), w1_half(far, side), w_send.at[3], w_recv.at[3], to_side)
@@ -186,15 +211,12 @@
             return pltpu.make_async_copy(xc.at[n % SLOT_X, :, pl.ds(2, WIN)], x_rest.at[n - now], rest_sem.at[n - now, 0])
         return pltpu.make_async_copy(hx.at[n % SLOT_H], h_rest.at[n - now], rest_sem.at[n - now, 1])
 
-    def last(i):
-        return jnp.clip(i + 6 + jnp.maximum(i, 0) // 4, -1, images - 1)
+    def seen(i):
+        return i + 2 + jnp.maximum(i - 9, 0) // 4
 
     def each(i, run):
-        lo, hi = last(i - 1), last(i)
-
-        @pl.when(hi > lo)
-        def _():
-            run(lo + 1)
+        lo, hi = seen(i - 1), seen(i)
+        run(lo + 1)
 
         @pl.when(hi > lo + 1)
         def _():
@@ -236,30 +258,35 @@
             rest_copy(n, 0).start()
             rest_copy(n, 1).start()
 
+    def part_copy(n):
+        return remote(xc.at[n % SLOT_X, chip, pl.ds(2, WIN), pl.ds(edge, EDGE), :], hp.at[n], p_send.at[n], p_recv.at[n], to_side)
+
     def control(i):
-        each(i, start_a)
-        each(i - 2, start_x)
-        each(i - 1, wait_a)
-
-        @pl.when(last(i - 1) > last(i - 2) + 1)
-        def _():
-            do_merge(last(i - 1) - 1, True)
-        each(i - 4, start_h)
-        each(i - 5, wait_h)
-
-    def release(i):
-        def free_a(n):
-            @pl.when(n < images - SLOT_A)
-            def _():
-                pl.semaphore_signal(credit_a, inc=1, device_id=to_mate, device_id_type=MESH)
-        each(i - 1, free_a)
-        built = i + 1
-
-        @pl.when(jnp.logical_and(built >= 0, built < images - SLOT_X))
+        @pl.when(i + EARLY + 1 < images)
+        def _():
+            start_a(i + EARLY + 1)
+
+        @pl.when(jnp.logical_and(i >= 1, i + EARLY - 1 < images))
+        def _():
+            start_x(i + EARLY - 1)
+
+        @pl.when(i + EARLY < images)
+        def _():
+            wait_a(i + EARLY)
+        each(i, start_h)
+        each(i - 1, wait_h)
+
+    def free_a(n):
+        @pl.when(n < images - SLOT_A)
+        def _():
+            pl.semaphore_signal(credit_a, inc=1, device_id=to_mate, device_id_type=MESH)
+
+    def free_built(n):
+        @pl.when(n < images - SLOT_X)
         def _():
             pl.semaphore_signal(credit_x, inc=1, device_id=to_far, device_id_type=MESH)
 
-        @pl.when(jnp.logical_and(built >= 0, built < images - SLOT_H))
+        @pl.when(n < images - SLOT_H)
         def _():
             pl.semaphore_signal(credit_h, inc=1, device_id=to_side, device_id_type=MESH)
 
@@ -274,55 +301,91 @@
     w_own.start()
     w2_own.start()
 
+    for n in range(3):
+        start_a(n)
+    w_own.wait()
+    w_mate.wait()
+
     def fill(t, _):
-        i = t - 6
-
-        @pl.when(i == -2)
+        @pl.when(t < EARLY)
+        def _():
+            wait_a(t)
+
+        @pl.when(jnp.logical_and(t >= 1, t <= EARLY))
+        def _():
+            start_x(t - 1)
+            part_copy(t - 1).start()
+
+        @pl.when(t + 3 <= EARLY)
+        def _():
+            start_a(t + 3)
+
+        @pl.when(t < EARLY)
+        def _():
+            do_merge(t, True)
+            free_a(t)
+
+        @pl.when(t == 4)
         def _():
             w_far.wait()
             w_side.start()
             w_pass[0].start()
 
-        @pl.when(i == -1)
+        @pl.when(t == 8)
         def _():
             w_side.wait()
             w_pass[1].start()
-        control(i)
-
-        @pl.when(last(i - 1) > last(i - 2))
-        def _():
-            do_merge(last(i - 1), True)
-
-        @pl.when(i + 1 >= 0)
-        def _():
-            do_build(i + 1)
-        release(i)
+
+        @pl.when(t == 9)
+        def _():
+            start_h(0)
+
+        @pl.when(t == EARLY + 1)
+        def _():
+            start_h(1)
+
+        @pl.when(t >= 2)
+        def _():
+            n = t - 2
+            part_copy(n).wait()
+            build_half(is_left, xc.at[n % SLOT_X, chip], hp.at[n], x3.at[chip], xh.at[chip])
+            conv1_part(x3.at[chip], xh.at[chip], w1v.at[chip], zp.at[n])
         return 0
 
-    lax.fori_loop(0, 6, fill, 0)
-    w_mate.wait()
-    w_own.wait()
+    lax.fori_loop(0, EARLY + 2, fill, 0)
     w2_own.wait()
     for copy in w_pass:
         copy.wait()
+    wait_h(0)
+    do_build(0)
+    free_built(0)
     w_out = pltpu.make_async_copy(w1v, w1_all, w_loc.at[2])
     w_out.start()
 
-    def step(i, _):
+    def step(early, i, _):
         control(i)
 
         @pl.when(i >= 2)
         def _():
             out_copy(i - 2).wait()
-        conv1(is_left, model == 0, model == 3, x3, xh, w1v, b1, y3)
+        if early:
+            conv1(is_left, model == 0, model == 3, [x3.at[1 - chip]], [xh.at[1 - chip]], w1v.at[1 - chip], 1152, b1, y3, zp.at[i])
+        else:
+            conv1(is_left, model == 0, model == 3, [x3.at[0], x3.at[1]], [xh.at[0], xh.at[1]], w1v, 2304, b1, y3)
         do_build(i + 1)
-        do_merge(last(i - 1), last(i - 1) > last(i - 2))
+        do_merge(i + EARLY, i + EARLY < images)
         conv2(y3, w2v, b2, ob.at[i % 2])
         out_copy(i).start()
-        release(i)
+
+        @pl.when(i + EARLY < images)
+        def _():
+            free_a(i + EARLY)
+        free_built(i + 1)
         return 0
 
-    lax.fori_loop(0, now, step, 0)
+    lax.fori_loop(0, EARLY, functools.partial(step, True), 0)
+    lax.fori_loop(EARLY, now, functools.partial(step, False), 0)
+    each(now - 1, wait_h)
     out_copy(now - 2).wait()
     out_copy(now - 1).wait()
     w_out.wait()
@@ -377,7 +440,7 @@
         @pl.when(i >= 2)
         def _():
             out_copy(i - 2).wait()
-        conv1(is_left, model == 0, model == 3, x3, xh, w1v, b1, y3)
+        conv1(is_left, model == 0, model == 3, [x3.at[0], x3.at[1]], [xh.at[0], xh.at[1]], w1v, 2304, b1, y3)
         n = jnp.minimum(i + 1, LATER - 1)
         build_x3(is_left, xc.at[n], hx.at[n], x3, xh)
         conv2(y3, w2v, b2, ob.at[i % 2])
@@ -404,11 +467,11 @@
         scratch_shapes=[
             pltpu.VMEM((LATER, 2, WIN + 4, COLS, 128), bf16),
             pltpu.VMEM((LATER, 2, WIN, EDGE, 128), bf16),
-            pltpu.VMEM((WIN * COLS, 768), bf16),
-            pltpu.VMEM((40, 768), jnp.float32),
+            pltpu.VMEM((2, WIN * COLS, 384), bf16),
+            pltpu.VMEM((2, 40, 384), jnp.float32),
             pltpu.VMEM(((ROWS + 2) * COLS, 1536), bf16),
             pltpu.VMEM((2, ROWS * COLS, 512), jnp.float32),
-            pltpu.VMEM((9, 256, 512), bf16),
+            pltpu.VMEM((2, 9, 128, 512), bf16),
             pltpu.VMEM((4608, 512), bf16),
             pltpu.VMEM((2, size, ROWS * COLS, 512), jnp.float32),
             dma((LATER, 2)), dma((2,)), dma((2,)), dma((2, size)), dma((2, size)),
@@ -429,7 +492,7 @@
             jax.ShapeDtypeStruct((images - LATER, ROWS * COLS, 512), jnp.float32),
             jax.ShapeDtypeStruct((LATER, 2, WIN, COLS, 128), bf16),
             jax.ShapeDtypeStruct((LATER, 2, WIN, EDGE, 128), bf16),
-            jax.ShapeDtypeStruct((9, 256, 512), bf16),
+            jax.ShapeDtypeStruct((2, 9, 128, 512), bf16),
         ],
         in_specs=[hbm, hbm, vmem, hbm, vmem],
         out_specs=[hbm] * 4,
@@ -438,15 +501,17 @@
             pltpu.VMEM((SLOT_S + 1, WIN, COLS, 128), bf16),
             pltpu.VMEM((SLOT_X + 1, 2, WIN + 4, COLS, 128), bf16),
             pltpu.VMEM((SLOT_H, 2, WIN, EDGE, 128), bf16),
-            pltpu.VMEM((WIN * COLS, 768), bf16),
-            pltpu.VMEM((40, 768), jnp.float32),
+            pltpu.VMEM((2, WIN * COLS, 384), bf16),
+            pltpu.VMEM((2, 40, 384), jnp.float32),
             pltpu.VMEM(((ROWS + 2) * COLS, 1536), bf16),
             pltpu.VMEM((2, ROWS * COLS, 512), jnp.float32),
-            pltpu.VMEM((9, 256, 512), bf16),
+            pltpu.VMEM((2, 9, 128, 512), bf16),
             pltpu.VMEM((4608, 512), bf16),
+            pltpu.VMEM((EARLY, WIN, EDGE, 128), bf16),
+            pltpu.VMEM((EARLY, HALO + (ROWS + 2) * COLS, 512), bf16),
             dma((SLOT_A, 2)), dma((SLOT_A, 2)), dma((SLOT_A, 2)),
             dma((SLOT_X,)), dma((SLOT_X,)), dma((SLOT_H,)), dma((SLOT_H,)), dma((2,)),
-            dma((3,)), dma((5,)), dma((5,)), dma((LATER, 2)),
+            dma((3,)), dma((5,)), dma((5,)), dma((LATER, 2)), dma((EARLY,)), dma((EARLY,)),
             pltpu.SemaphoreType.REGULAR, pltpu.SemaphoreType.REGULAR, pltpu.SemaphoreType.REGULAR,
         ],
         compiler_params=pltpu.CompilerParams(vmem_limit_bytes=60 * 1024 * 1024, collective_id=0, has_side_effects=True),

time: 305 us -> 305 us (level)
  no operation moved by 1% of the time
where the time goes in v5:
time: 305 us
  Pallas kernels  304 us (100%)
    pallas_call x1, Pallas kernels, fused(): pl.pallas_call(functools.partial(fused_kernel, images), out_shape=[jax.Sh...  248 us
    pallas_call x1, Pallas kernels, rest(): pl.pallas_call(functools.partial(rest_kernel, images), out_shape=jax.Shap...  56.1 us

profile of v5, /device:TPU:0, one launch (start us, length us, event | category | flops | bytes accessed | tf_op | source)
XLA Modules:
  0.0 304.7 jit_solution(6417573706539784840)
XLA Ops:
  0.0 248.3 %shard_map.55 = (f32[26,1024,512]{2,1,0:T(8,128)}, bf16[6,2,20,64,128]{4,3,2,1,0:T(8,128)(2,1)}, bf16[6,2,20,8,128]{4,3,2,1,0:T(8,128)(2,1)}, bf16[2,9,128,512]{3,2,1,0:T(8,128)(2,1)}) custom-call(bf16[32,64,64,64]{3,2,1,0:T(8,128)(2,1)} %x.1, bf16[9,64,512]{2,1,0:T(8,128)(2,1)} %bitcast.7, f32[1,512]{1,0:T(1,128)} %bitcast.8, bf16[4608,512]{1,0:T(8,128)(2,1)} %bitcast.5, ...), custom_call_target="tpu_custom_call" | custom-call | tf_op jit(solution)/shard_map/pallas_call | solution.py:489
  248.4 56.1 %shard_map.56 = f32[32,1024,512]{2,1,0:T(8,128)} custom-call(f32[26,1024,512]{2,1,0:T(8,128)} %get-tuple-element.9.y_done, bf16[6,2,20,64,128]{4,3,2,1,0:T(8,128)(2,1)} %get-tuple-element.10.x_rest, bf16[6,2,20,8,128]{4,3,2,1,0:T(8,128)(2,1)} %get-tuple-element.11.h_rest, bf16[2,9,128,512]{3,2,1,0:T(8,128)(2,1)} %get-tuple-element.12.w1, f32[1,512]{1,0:T(1,128)} %bitcast.9, ...), custom_call_target="tpu_custom_call" | custom-call | tf_op jit(solution)/shard_map/pallas_call | solution.py:462

commit v6 on v5

--- a/solution.py
+++ b/solution.py
@@ -16,7 +16,7 @@
 SLOT_S = 10
 SLOT_X = 12
 SLOT_H = 8
-LATER = 6
+LATER = 5
 EARLY = 10
 HALO = 32
 
@@ -212,7 +212,7 @@
         return pltpu.make_async_copy(hx.at[n % SLOT_H], h_rest.at[n - now], rest_sem.at[n - now, 1])
 
     def seen(i):
-        return i + 2 + jnp.maximum(i - 9, 0) // 4
+        return i + 2 + jnp.maximum(i - 10, 0) // 8
 
     def each(i, run):
         lo, hi = seen(i - 1), seen(i)
@@ -385,7 +385,10 @@
 
     lax.fori_loop(0, EARLY, functools.partial(step, True), 0)
     lax.fori_loop(EARLY, now, functools.partial(step, False), 0)
+    late = images - 1
+    start_h(late)
     each(now - 1, wait_h)
+    wait_h(late)
     out_copy(now - 2).wait()
     out_copy(now - 1).wait()
     w_out.wait()

time: 305 us -> 315 us (1.033)
  Pallas kernels: 304 us -> 315 us
    pallas_call x1, Pallas kernels: 248 us -> 259 us  [fused(): pl.pallas_call(functools.partial(fused_kernel, images), out_shape=[jax.Sh...]
where the time goes in v6:
time: 315 us
  Pallas kernels  315 us (100%)
    pallas_call x1, Pallas kernels, fused(): pl.pallas_call(functools.partial(fused_kernel, images), out_shape=[jax.Sh...  259 us
    pallas_call x1, Pallas kernels, rest(): pl.pallas_call(functools.partial(rest_kernel, images), out_shape=jax.Shap...  55.5 us

profile of v6, /device:TPU:0, one launch (start us, length us, event | category | flops | bytes accessed | tf_op | source)
XLA Modules:
  0.0 314.8 jit_solution(6731875726349821495)
XLA Ops:
  0.0 259.2 %shard_map.55 = (f32[27,1024,512]{2,1,0:T(8,128)}, bf16[5,2,20,64,128]{4,3,2,1,0:T(8,128)(2,1)}, bf16[5,2,20,8,128]{4,3,2,1,0:T(8,128)(2,1)}, bf16[2,9,128,512]{3,2,1,0:T(8,128)(2,1)}) custom-call(bf16[32,64,64,64]{3,2,1,0:T(8,128)(2,1)} %x.1, bf16[9,64,512]{2,1,0:T(8,128)(2,1)} %bitcast.7, f32[1,512]{1,0:T(1,128)} %bitcast.8, bf16[4608,512]{1,0:T(8,128)(2,1)} %bitcast.5, ...), custom_call_target="tpu_custom_call" | custom-call | tf_op jit(solution)/shard_map/pallas_call | solution.py:492
  259.2 55.5 %shard_map.56 = f32[32,1024,512]{2,1,0:T(8,128)} custom-call(f32[27,1024,512]{2,1,0:T(8,128)} %get-tuple-element.9.y_done, bf16[5,2,20,64,128]{4,3,2,1,0:T(8,128)(2,1)} %get-tuple-element.10.x_rest, bf16[5,2,20,8,128]{4,3,2,1,0:T(8,128)(2,1)} %get-tuple-element.11.h_rest, bf16[2,9,128,512]{3,2,1,0:T(8,128)(2,1)} %get-tuple-element.12.w1, f32[1,512]{1,0:T(1,128)} %bitcast.9, ...), custom_call_target="tpu_custom_call" | custom-call | tf_op jit(solution)/shard_map/pallas_call | solution.py:465

commit v7 on v5

--- a/solution.py
+++ b/solution.py
@@ -17,7 +17,7 @@
 SLOT_X = 12
 SLOT_H = 8
 LATER = 6
-EARLY = 10
+EARLY = 11
 HALO = 32
 
 
@@ -165,9 +165,12 @@
         return w1v.at[m // 2, :, pl.ds(pl.multiple_of(m % 2 * 64, 64), 64), pl.ds(pl.multiple_of(half * 256, 256), 256)]
 
     w_far = remote(w1.at[:, :, pl.ds(pl.multiple_of(side * 256, 256), 256)], w1_half(model, side), w_send.at[0], w_recv.at[0], to_far)
-    w_side = remote(w1_half(far, side), w1_half(far, side), w_send.at[3], w_recv.at[3], to_side)
-    w_pass = [remote(w1_half(far, half), w1_half(far, half), w_send.at[2 + 2 * t], w_recv.at[2 + 2 * t], to_mate)
-              for t, half in enumerate((side, 1 - side))]
+    def w1_piece(half, piece):
+        return w1_half(far, half).at[pl.ds(3 * piece, 3)]
+
+    w_side = [remote(w1_piece(side, p), w1_piece(side, p), w_send.at[3 + p], w_recv.at[3 + p], to_side) for p in range(3)]
+    w_pass = remote(w1_half(far, side), w1_half(far, side), w_send.at[2], w_recv.at[2], to_mate)
+    w_last = [remote(w1_piece(1 - side, p), w1_piece(1 - side, p), w_send.at[6 + p], w_recv.at[6 + p], to_mate) for p in range(3)]
     w_mate = remote(w1, w1_part(model), w_send.at[1], w_recv.at[1], to_mate)
     w_own = pltpu.make_async_copy(w1, w1_part(model), w_loc.at[0])
     w2_own = pltpu.make_async_copy(w2, w2v, w_loc.at[1])
@@ -212,7 +215,7 @@
         return pltpu.make_async_copy(hx.at[n % SLOT_H], h_rest.at[n - now], rest_sem.at[n - now, 1])
 
     def seen(i):
-        return i + 2 + jnp.maximum(i - 9, 0) // 4
+        return i + 2 + jnp.maximum(i - 12, 0) // 6
 
     def each(i, run):
         lo, hi = seen(i - 1), seen(i)
@@ -320,41 +323,57 @@
         def _():
             start_a(t + 3)
 
+        @pl.when(t == 5)
+        def _():
+            w_far.wait()
+            w_pass.start()
+        for p in range(3):
+            @pl.when(t == 5 + p)
+            def _():
+                w_side[p].start()
+
+            @pl.when(t == 7 + p)
+            def _():
+                w_side[p].wait()
+                w_last[p].start()
+
+        @pl.when(t == 9)
+        def _():
+            start_h(0)
+
+        @pl.when(t == EARLY + 2)
+        def _():
+            start_h(1)
+
+        @pl.when(jnp.logical_and(t >= 2, t < EARLY + 2))
+        def _():
+            part_copy(t - 2).wait()
+
+        def build_part(n):
+            build_half(is_left, xc.at[n % SLOT_X, chip], hp.at[n], x3.at[chip], xh.at[chip])
+
+        @pl.when(t < 3)
+        def _():
+            do_merge(t, True)
+
+        @pl.when(t == 2)
+        def _():
+            build_part(0)
+
+        @pl.when(t >= 3)
+        def _():
+            conv1_part(x3.at[chip], xh.at[chip], w1v.at[chip], zp.at[t - 3])
+            build_part(jnp.minimum(t - 2, EARLY - 1))
+            do_merge(jnp.minimum(t, EARLY - 1), t < EARLY)
+
         @pl.when(t < EARLY)
         def _():
-            do_merge(t, True)
             free_a(t)
-
-        @pl.when(t == 4)
-        def _():
-            w_far.wait()
-            w_side.start()
-            w_pass[0].start()
-
-        @pl.when(t == 8)
-        def _():
-            w_side.wait()
-            w_pass[1].start()
-
-        @pl.when(t == 9)
-        def _():
-            start_h(0)
-
-        @pl.when(t == EARLY + 1)
-        def _():
-            start_h(1)
-
-        @pl.when(t >= 2)
-        def _():
-            n = t - 2
-            part_copy(n).wait()
-            build_half(is_left, xc.at[n % SLOT_X, chip], hp.at[n], x3.at[chip], xh.at[chip])
-            conv1_part(x3.at[chip], xh.at[chip], w1v.at[chip], zp.at[n])
         return 0
 
-    lax.fori_loop(0, EARLY + 2, fill, 0)
+    lax.fori_loop(0, EARLY + 3, fill, 0)
     w2_own.wait()
-    for copy in w_pass:
+    for copy in [w_pass] + w_last:
         copy.wait()
     wait_h(0)
     do_build(0)
@@ -385,7 +404,11 @@
 
     lax.fori_loop(0, EARLY, functools.partial(step, True), 0)
     lax.fori_loop(EARLY, now, functools.partial(step, False), 0)
+    for n in range(images - 2, images):
+        start_h(n)
     each(now - 1, wait_h)
+    for n in range(images - 2, images):
+        wait_h(n)
     out_copy(now - 2).wait()
     out_copy(now - 1).wait()
     w_out.wait()
@@ -511,7 +534,7 @@
             pltpu.VMEM((EARLY, HALO + (ROWS + 2) * COLS, 512), bf16),
             dma((SLOT_A, 2)), dma((SLOT_A, 2)), dma((SLOT_A, 2)),
             dma((SLOT_X,)), dma((SLOT_X,)), dma((SLOT_H,)), dma((SLOT_H,)), dma((2,)),
-            dma((3,)), dma((5,)), dma((5,)), dma((LATER, 2)), dma((EARLY,)), dma((EARLY,)),
+            dma((3,)), dma((9,)), dma((9,)), dma((LATER, 2)), dma((EARLY,)), dma((EARLY,)),
             pltpu.SemaphoreType.REGULAR, pltpu.SemaphoreType.REGULAR, pltpu.SemaphoreType.REGULAR,
         ],
         compiler_params=pltpu.CompilerParams(vmem_limit_bytes=60 * 1024 * 1024, collective_id=0, has_side_effects=True),

time: 305 us -> 308 us (level)
  no operation moved by 1% of the time
where the time goes in v7:
time: 308 us; the launch traced here: 307 us
  Pallas kernels  307 us (100%)
    pallas_call x1, Pallas kernels, fused(): pl.pallas_call(functools.partial(fused_kernel, images), out_shape=[jax.Sh...  251 us
    pallas_call x1, Pallas kernels, rest(): pl.pallas_call(functools.partial(rest_kernel, images), out_shape=jax.Shap...  56.1 us

profile of v7, /device:TPU:0, one launch (start us, length us, event | category | flops | bytes accessed | tf_op | source)
XLA Modules:
  0.0 307.5 jit_solution(101040656659194383)
XLA Ops:
  0.0 251.2 %shard_map.55 = (f32[26,1024,512]{2,1,0:T(8,128)}, bf16[6,2,20,64,128]{4,3,2,1,0:T(8,128)(2,1)}, bf16[6,2,20,8,128]{4,3,2,1,0:T(8,128)(2,1)}, bf16[2,9,128,512]{3,2,1,0:T(8,128)(2,1)}) custom-call(bf16[32,64,64,64]{3,2,1,0:T(8,128)(2,1)} %x.1, bf16[9,64,512]{2,1,0:T(8,128)(2,1)} %bitcast.7, f32[1,512]{1,0:T(1,128)} %bitcast.8, bf16[4608,512]{1,0:T(8,128)(2,1)} %bitcast.5, ...), custom_call_target="tpu_custom_call" | custom-call | tf_op jit(solution)/shard_map/pallas_call | solution.py:512
  251.2 56.1 %shard_map.56 = f32[32,1024,512]{2,1,0:T(8,128)} custom-call(f32[26,1024,512]{2,1,0:T(8,128)} %get-tuple-element.9.y_done, bf16[6,2,20,64,128]{4,3,2,1,0:T(8,128)(2,1)} %get-tuple-element.10.x_rest, bf16[6,2,20,8,128]{4,3,2,1,0:T(8,128)(2,1)} %get-tuple-element.11.h_rest, bf16[2,9,128,512]{3,2,1,0:T(8,128)(2,1)} %get-tuple-element.12.w1, f32[1,512]{1,0:T(1,128)} %bitcast.9, ...), custom_call_target="tpu_custom_call" | custom-call | tf_op jit(solution)/shard_map/pallas_call | solution.py:485

commit v8 on v7

--- a/solution.py
+++ b/solution.py
@@ -17,7 +17,7 @@
 SLOT_X = 12
 SLOT_H = 8
 LATER = 6
-EARLY = 11
+EARLY = 6
 HALO = 32
 
 
@@ -215,11 +215,25 @@
         return pltpu.make_async_copy(hx.at[n % SLOT_H], h_rest.at[n - now], rest_sem.at[n - now, 1])
 
     def seen(i):
-        return i + 2 + jnp.maximum(i - 12, 0) // 6
+        return i + 2 + jnp.maximum(i - 10, 0) // 5
 
     def each(i, run):
         lo, hi = seen(i - 1), seen(i)
         run(lo + 1)
+
+        @pl.when(hi > lo + 1)
+        def _():
+            run(lo + 2)
+
+    def last(i):
+        return jnp.minimum(i + EARLY + 1 + jnp.maximum(i, 0) // 4, images - 1)
+
+    def batch(i, run):
+        lo, hi = last(i - 1), last(i)
+
+        @pl.when(hi > lo)
+        def _():
+            run(lo + 1)
 
         @pl.when(hi > lo + 1)
         def _():
@@ -265,17 +279,16 @@
         return remote(xc.at[n % SLOT_X, chip, pl.ds(2, WIN), pl.ds(edge, EDGE), :], hp.at[n], p_send.at[n], p_recv.at[n], to_side)
 
     def control(i):
-        @pl.when(i + EARLY + 1 < images)
-        def _():
-            start_a(i + EARLY + 1)
-
-        @pl.when(jnp.logical_and(i >= 1, i + EARLY - 1 < images))
-        def _():
-            start_x(i + EARLY - 1)
-
-        @pl.when(i + EARLY < images)
-        def _():
-            wait_a(i + EARLY)
+        batch(i, start_a)
+
+        @pl.when(i >= 1)
+        def _():
+            batch(i - 2, start_x)
+        batch(i - 1, wait_a)
+
+        @pl.when(last(i - 1) > last(i - 2) + 1)
+        def _():
+            do_merge(last(i - 1) - 1, True)
         each(i, start_h)
         each(i - 1, wait_h)
 
@@ -323,21 +336,22 @@
         def _():
             start_a(t + 3)
 
-        @pl.when(t == 5)
+        @pl.when(t == 3)
         def _():
             w_far.wait()
             w_pass.start()
+
+        @pl.when(t == EARLY + 2)
+        def _():
+            for p in range(3):
+                w_side[p].wait()
+                w_last[p].start()
         for p in range(3):
-            @pl.when(t == 5 + p)
+            @pl.when(t == 3 + p)
             def _():
                 w_side[p].start()
 
-            @pl.when(t == 7 + p)
-            def _():
-                w_side[p].wait()
-                w_last[p].start()
-
-        @pl.when(t == 9)
+        @pl.when(t == EARLY + 1)
         def _():
             start_h(0)
 
@@ -392,23 +406,20 @@
         else:
             conv1(is_left, model == 0, model == 3, [x3.at[0], x3.at[1]], [xh.at[0], xh.at[1]], w1v, 2304, b1, y3)
         do_build(i + 1)
-        do_merge(i + EARLY, i + EARLY < images)
+        do_merge(last(i - 1), last(i - 1) > last(i - 2))
         conv2(y3, w2v, b2, ob.at[i % 2])
         out_copy(i).start()
 
-        @pl.when(i + EARLY < images)
-        def _():
-            free_a(i + EARLY)
+        batch(i - 1, free_a)
         free_built(i + 1)
         return 0
 
     lax.fori_loop(0, EARLY, functools.partial(step, True), 0)
     lax.fori_loop(EARLY, now, functools.partial(step, False), 0)
-    for n in range(images - 2, images):
-        start_h(n)
+    late = images - 1
+    start_h(late)
     each(now - 1, wait_h)
-    for n in range(images - 2, images):
-        wait_h(n)
+    wait_h(late)
     out_copy(now - 2).wait()
     out_copy(now - 1).wait()
     w_out.wait()

time: 308 us -> 306 us (level)
  no operation moved by 1% of the time
where the time goes in v8:
time: 306 us
  Pallas kernels  306 us (100%)
    pallas_call x1, Pallas kernels, fused(): pl.pallas_call(functools.partial(fused_kernel, images), out_shape=[jax.Sh...  250 us
    pallas_call x1, Pallas kernels, rest(): pl.pallas_call(functools.partial(rest_kernel, images), out_shape=jax.Shap...  56.2 us

profile of v8, /device:TPU:0, one launch (start us, length us, event | category | flops | bytes accessed | tf_op | source)
XLA Modules:
  0.0 305.9 jit_solution(14703876629598646612)
XLA Ops:
  0.0 249.5 %shard_map.55 = (f32[26,1024,512]{2,1,0:T(8,128)}, bf16[6,2,20,64,128]{4,3,2,1,0:T(8,128)(2,1)}, bf16[6,2,20,8,128]{4,3,2,1,0:T(8,128)(2,1)}, bf16[2,9,128,512]{3,2,1,0:T(8,128)(2,1)}) custom-call(bf16[32,64,64,64]{3,2,1,0:T(8,128)(2,1)} %x.1, bf16[9,64,512]{2,1,0:T(8,128)(2,1)} %bitcast.7, f32[1,512]{1,0:T(1,128)} %bitcast.8, bf16[4608,512]{1,0:T(8,128)(2,1)} %bitcast.5, ...), custom_call_target="tpu_custom_call" | custom-call | tf_op jit(solution)/shard_map/pallas_call | solution.py:523
  249.5 56.2 %shard_map.56 = f32[32,1024,512]{2,1,0:T(8,128)} custom-call(f32[26,1024,512]{2,1,0:T(8,128)} %get-tuple-element.9.y_done, bf16[6,2,20,64,128]{4,3,2,1,0:T(8,128)(2,1)} %get-tuple-element.10.x_rest, bf16[6,2,20,8,128]{4,3,2,1,0:T(8,128)(2,1)} %get-tuple-element.11.h_rest, bf16[2,9,128,512]{3,2,1,0:T(8,128)(2,1)} %get-tuple-element.12.w1, f32[1,512]{1,0:T(1,128)} %bitcast.9, ...), custom_call_target="tpu_custom_call" | custom-call | tf_op jit(solution)/shard_map/pallas_call | solution.py:496

commit v9 on v8

--- a/solution.py
+++ b/solution.py
@@ -17,7 +17,7 @@
 SLOT_X = 12
 SLOT_H = 8
 LATER = 6
-EARLY = 6
+EARLY = 5
 HALO = 32
 
 
@@ -215,7 +215,7 @@
         return pltpu.make_async_copy(hx.at[n % SLOT_H], h_rest.at[n - now], rest_sem.at[n - now, 1])
 
     def seen(i):
-        return i + 2 + jnp.maximum(i - 10, 0) // 5
+        return i + 2 + jnp.maximum(i - 9, 0) // 4
 
     def each(i, run):
         lo, hi = seen(i - 1), seen(i)
@@ -336,7 +336,7 @@
         def _():
             start_a(t + 3)
 
-        @pl.when(t == 3)
+        @pl.when(t == 2)
         def _():
             w_far.wait()
             w_pass.start()
@@ -347,7 +347,7 @@
                 w_side[p].wait()
                 w_last[p].start()
         for p in range(3):
-            @pl.when(t == 3 + p)
+            @pl.when(t == 2 + p)
             def _():
                 w_side[p].start()
 
@@ -416,10 +416,7 @@
 
     lax.fori_loop(0, EARLY, functools.partial(step, True), 0)
     lax.fori_loop(EARLY, now, functools.partial(step, False), 0)
-    late = images - 1
-    start_h(late)
     each(now - 1, wait_h)
-    wait_h(late)
     out_copy(now - 2).wait()
     out_copy(now - 1).wait()
     w_out.wait()
@@ -462,10 +459,15 @@
     for copy in load(0):
         copy.wait()
     build_x3(is_left, xc.at[0], hx.at[0], x3, xh)
-    for copy in weights + [c for n in range(1, LATER) for c in load(n)]:
+    for copy in weights:
         copy.wait()
 
     def step(i, _):
+        for n in range(1, LATER):
+            @pl.when(i == n - 1)
+            def _():
+                for copy in load(n):
+                    copy.wait()
         each(i - 1, lambda s, q: bring(s, q).wait())
         each(i - 1, lambda s, q: put(s, q).start())
         each(i - 2, lambda s, q: put(s, q).wait())

time: 306 us -> 303 us (level)
  no operation moved by 1% of the time
where the time goes in v9:
time: 303 us
  Pallas kernels  303 us (100%)
    pallas_call x1, Pallas kernels, fused(): pl.pallas_call(functools.partial(fused_kernel, images), out_shape=[jax.Sh...  247 us
    pallas_call x1, Pallas kernels, rest(): pl.pallas_call(functools.partial(rest_kernel, images), out_shape=jax.Shap...  56.1 us

profile of v9, /device:TPU:0, one launch (start us, length us, event | category | flops | bytes accessed | tf_op | source)
XLA Modules:
  0.0 303.4 jit_solution(9876246308070901092)
XLA Ops:
  0.0 247.1 %shard_map.55 = (f32[26,1024,512]{2,1,0:T(8,128)}, bf16[6,2,20,64,128]{4,3,2,1,0:T(8,128)(2,1)}, bf16[6,2,20,8,128]{4,3,2,1,0:T(8,128)(2,1)}, bf16[2,9,128,512]{3,2,1,0:T(8,128)(2,1)}) custom-call(bf16[32,64,64,64]{3,2,1,0:T(8,128)(2,1)} %x.1, bf16[9,64,512]{2,1,0:T(8,128)(2,1)} %bitcast.7, f32[1,512]{1,0:T(1,128)} %bitcast.8, bf16[4608,512]{1,0:T(8,128)(2,1)} %bitcast.5, ...), custom_call_target="tpu_custom_call" | custom-call | tf_op jit(solution)/shard_map/pallas_call | solution.py:525
  247.1 56.1 %shard_map.56 = f32[32,1024,512]{2,1,0:T(8,128)} custom-call(f32[26,1024,512]{2,1,0:T(8,128)} %get-tuple-element.9.y_done, bf16[6,2,20,64,128]{4,3,2,1,0:T(8,128)(2,1)} %get-tuple-element.10.x_rest, bf16[6,2,20,8,128]{4,3,2,1,0:T(8,128)(2,1)} %get-tuple-element.11.h_rest, bf16[2,9,128,512]{3,2,1,0:T(8,128)(2,1)} %get-tuple-element.12.w1, f32[1,512]{1,0:T(1,128)} %bitcast.9, ...), custom_call_target="tpu_custom_call" | custom-call | tf_op jit(solution)/shard_map/pallas_call | solution.py:498
